TPU v7x, 32 devices: a whole 2x2x4 slice. The times are simulated.
32 devices in a mesh: row: 16 (over z, x, core), col: 2 (over y).
Axes of the slice: x: 2, y: 2, z: 4, core: 2. Of those that a mesh axis runs over, the one named last changes fastest.
Arguments:
- features: bfloat16 [4096, 440], P(('row', 'col')), may hold values from -1 to 1
- coeffs: bfloat16 [4096, 144], P(('row', 'col')), may hold values from -0.375 to 0.375
- targets: float32 [4096, 144], P(('row', 'col')), may hold values from -6 to 6
Outputs:
- residual: float32 [4096, 144], P(('row', 'col'))
All inputs are finite; a program needn't handle non-finite values.
Results may differ from a plain program's by a relative error of at most 0.0012.
Values may be sent and summed in bfloat16 or wider, within the bound.
No kernel may reach another device: no remote copies, remote signals or barrier semaphores. Data moves between devices by JAX's collectives and lax.ppermute only.
A program may use at most 64 MiB of HBM per device.

v0:
```python
import functools
import math

import jax
import jax.numpy as jnp
from jax import lax
from jax.experimental import pallas as pl
from jax.experimental.pallas import tpu as pltpu
from jax.sharding import PartitionSpec as P

AXES = ("row", "col")
NEAR_BYTES = 2 << 20
LOG2E = math.log2(math.e)


def square_rows(wide, shift):
    sq = jnp.sum(wide * wide, axis=0, keepdims=True)
    high = sq.astype(jnp.bfloat16).astype(jnp.float32)
    mid = (sq - high).astype(jnp.bfloat16).astype(jnp.float32)
    low = (sq - high) - mid
    row = lax.broadcasted_iota(jnp.int32, (8, wide.shape[1]), 0)
    rest = jnp.where(row < 6, 1.0, 0.0)
    for n, part in enumerate((high, mid, low)):
        rest = jnp.where(row == shift + n, part, rest)
    return rest.astype(jnp.bfloat16)


def stacked(weights, values, near):
    outs, feats, width = weights.shape[0], values.shape[0], values.shape[1]

    def body(weight_ref, value_ref, out_ref):
        out_ref[:outs, :] = weight_ref[...]
        value = value_ref[...]
        out_ref[outs:outs + feats, :] = value
        out_ref[outs + feats:, :] = square_rows(value.astype(jnp.float32), 0)

    shape = (outs + feats + 8, width)
    vmem = pl.BlockSpec(memory_space=pltpu.VMEM)
    return pl.pallas_call(
        body,
        out_shape=pltpu.VMEM(shape, values.dtype) if near else jax.ShapeDtypeStruct(shape, values.dtype),
        in_specs=[vmem] * 2,
        out_specs=vmem,
        name="stacked",
    )(weights, values)


def products(work, outs, feats, kinds, near):
    arrays, slots = [], {}

    def slot(a):
        if id(a) not in slots:
            slots[id(a)] = len(arrays)
            arrays.append(a)
        return slots[id(a)]

    plan = [
        (slot(q), [slot(k) for k in keys], None if old is None else slot(old))
        for q, keys, old in work
    ]
    count = len(arrays)
    width = work[0][0].shape[1]

    def body(*refs):
        ins, out_refs, left_ref = refs[:count], refs[count:-1], refs[-1]
        for n, (q, _, _) in enumerate(plan):
            skip = outs if ins[q].shape[0] > feats else 0
            value = ins[q][skip:skip + feats, :]
            wide = value.astype(jnp.float32)
            left_ref[n, :feats, :] = (wide * -2.0).astype(jnp.bfloat16)
            left_ref[n, feats:, :] = square_rows(wide, 3)
        lhs = [left_ref[n].T for n in range(len(plan))]
        acc = [None if old is None else ins[old][...] for _, _, old in plan]
        groups = []
        for _, keys, _ in plan:
            for n in range(0, len(keys), 2):
                group = tuple(keys[n:n + 2])
                if group not in groups:
                    groups.append(group)
        for group in groups:
            rhs = jnp.concatenate([ins[k][outs:, :] for k in group], axis=1)
            weight = jnp.concatenate([ins[k][:outs, :] for k in group], axis=1)
            users = [i for i, (_, keys, _) in enumerate(plan) if group[0] in keys]
            left = jnp.concatenate([lhs[i] for i in users], axis=0)
            d2 = jnp.maximum(jnp.dot(left, rhs, preferred_element_type=jnp.float32), 1e-30)
            kern = jnp.exp2((d2 * -LOG2E) * lax.rsqrt(d2)).astype(jnp.bfloat16)
            part = lax.dot_general(
                weight, kern, (((1,), (1,)), ((), ())), preferred_element_type=jnp.float32
            )
            for n, i in enumerate(users):
                mine = part[:, n * width:(n + 1) * width]
                acc[i] = mine if acc[i] is None else acc[i] + mine
        for i in range(len(plan)):
            out_refs[i][...] = acc[i].astype(out_refs[i].dtype)

    shapes = [((outs, width), kind) for kind in kinds]
    vmem = pl.BlockSpec(memory_space=pltpu.VMEM)
    if near:
        arrays = [pltpu.with_memory_space_constraint(a, pltpu.VMEM) for a in arrays]
        shapes = [pltpu.VMEM(*s) for s in shapes]
    else:
        shapes = [jax.ShapeDtypeStruct(*s) for s in shapes]
    return pl.pallas_call(
        body,
        out_shape=shapes,
        in_specs=[vmem] * count,
        out_specs=[vmem] * len(work),
        scratch_shapes=[pltpu.VMEM((len(work), feats + 8, width), jnp.bfloat16)],
        name="products",
    )(*arrays)


def per_device(rows, cols, features, coeffs, targets):
    total = rows * cols
    core, xbit, z = cols, 2 * cols, 4 * cols
    f32, b16 = jnp.float32, jnp.bfloat16

    def swap(value, bits):
        return lax.ppermute(value, AXES, [(i, i ^ bits) for i in range(total)])

    mine = features.T
    outs = coeffs.shape[1]
    queries, order = [mine], [0]
    bit = rows // 8
    while bit >= 1:
        bits = bit * z
        queries = queries + [swap(q, bits) for q in queries]
        order = order + [o ^ bits for o in order]
        bit = bit // 2
    near = sum(a.size * a.dtype.itemsize for a in queries) * 8 <= NEAR_BYTES * 2
    both = stacked(coeffs.T, mine, near)
    queries[0] = both
    blocks = [both]
    for plane in reversed(range(1, 2 * cols)):
        bits = (plane // cols) * xbit + plane % cols
        blocks.append(swap(both, bits))
    keys = []
    for b in blocks:
        keys = keys + [b, swap(b, core)]

    feats = mine.shape[0]
    half = len(keys) // 2
    lead = queries[:-1] if len(queries) > 1 else queries
    early = products([(q, keys[:half], None) for q in lead], outs, feats, [f32] * len(lead), near)
    sent = [(q, keys[half:], e) for q, e in zip(lead, early)][1:]
    sent = sent + [(q, keys, None) for q in queries[len(lead):]]
    parts = products(sent, outs, feats, [b16] * len(sent), near) if sent else []
    own = products([(queries[0], keys[half:], early[0])], outs, feats, [f32], near)[0]
    result = own - targets.T
    for n, part in enumerate(parts):
        result = result + swap(part, order[n + 1]).astype(f32)
    return result.T


def solution(mesh):
    rows, cols = mesh.shape["row"], mesh.shape["col"]
    spec = P(AXES, None)
    body = functools.partial(per_device, rows, cols)
    return jax.shard_map(
        body, mesh=mesh, in_specs=(spec, spec, spec), out_specs=spec, check_vma=False
    )
```

profile of v0, /device:TPU:0, one launch (start us, length us, event | category | flops | bytes accessed | tf_op | source)
XLA Modules:
  0.0 29.7 jit_solution(9592429592477831551)
XLA Ops:
  0.0 0.0 copy-start
  0.0 1.1 %stacked.1.refs_0_.refs_9_ = bf16[592,128]{1,0:T(8,128)(2,1)S(1)} custom-call(bf16[144,128]{1,0:T(8,128)(2,1)} %bitcast.17, bf16[440,128]{1,0:T(8,128)(2,1)} %bitcast.14), custom_call_target="tpu_custom_call" | custom-call | tf_op jit(solution)/shard_map/stacked/pallas_call | solution.py:39
  1.1 4.0 %collective-permute-start.5 = (bf16[592,128]{1,0:T(8,128)(2,1)S(1)}, bf16[592,128]{1,0:T(8,128)(2,1)S(1)}, u32[]{:S(2)}, u32[]{:S(2)}) collective-permute-start(bf16[592,128]{1,0:T(8,128)(2,1)S(1)} %stacked.1.refs_0_.refs_9_), channel_id=1, source_target_pairs={{0,5},{1,4},{2,7},{3,6},{4,1},{5,0},{6,3},{7,2},{8,13},{9,12},{10,... | collective-permute-start | bytes 454664 | tf_op jit(solution)/shard_map/ppermute | solution.py:119
  5.0 0.5 %collective-permute-start = (bf16[592,128]{1,0:T(8,128)(2,1)S(1)}, bf16[592,128]{1,0:T(8,128)(2,1)S(1)}, u32[]{:S(2)}, u32[]{:S(2)}) collective-permute-start(bf16[592,128]{1,0:T(8,128)(2,1)S(1)} %stacked.1.refs_0_.refs_9_), channel_id=1, source_target_pairs={{0,4},{1,5},{2,6},{3,7},{4,0},{5,1},{6,2},{7,3},{8,12},{9,13},{10,... | collective-permute-start | bytes 454664 | tf_op jit(solution)/shard_map/ppermute | solution.py:119
  5.6 0.1 collective-permute-start.2
  5.7 0.0 copy-done
  5.7 3.0 %collective-permute-start.7 = (bf16[440,128]{1,0:T(8,128)(2,1)S(1)}, bf16[440,128]{1,0:T(8,128)(2,1)S(1)}, u32[]{:S(2)}, u32[]{:S(2)}) collective-permute-start(bf16[440,128]{1,0:T(8,128)(2,1)S(1)} %bitcast.15), channel_id=1, source_target_pairs={{0,16},{1,17},{2,18},{3,19},{4,20},{5,21},{6,22},{7,23},{8,24},{9,... | collective-permute-start | bytes 337928 | tf_op jit(solution)/shard_map/ppermute | solution.py:119
  8.7 1.6 %collective-permute-start.8 = (bf16[440,128]{1,0:T(8,128)(2,1)S(1)}, bf16[440,128]{1,0:T(8,128)(2,1)S(1)}, u32[]{:S(2)}, u32[]{:S(2)}) collective-permute-start(bf16[440,128]{1,0:T(8,128)(2,1)S(1)} %bitcast.16), channel_id=1, source_target_pairs={{0,8},{1,9},{2,10},{3,11},{4,12},{5,13},{6,14},{7,15},{8,0},{9,1},... | collective-permute-start | bytes 337928 | tf_op jit(solution)/shard_map/ppermute | solution.py:119
  10.2 2.4 %collective-permute-done.7.refs_4_.refs_0_ = bf16[440,128]{1,0:T(8,128)(2,1)S(1)} collective-permute-done((bf16[440,128]{1,0:T(8,128)(2,1)S(1)}, bf16[440,128]{1,0:T(8,128)(2,1)S(1)}, u32[]{:S(2)}, u32[]{:S(2)}) %collective-permute-start.7) | collective-permute-done | bytes 112672 | tf_op jit(solution)/shard_map/ppermute | solution.py:119
  12.6 0.0 collective-permute-start.4
  12.6 0.0 collective-permute-done.5.refs_2_.refs_11_
  12.6 0.5 %collective-permute-start.6 = (bf16[592,128]{1,0:T(8,128)(2,1)S(1)}, bf16[592,128]{1,0:T(8,128)(2,1)S(1)}, u32[]{:S(2)}, u32[]{:S(2)}) collective-permute-start(bf16[592,128]{1,0:T(8,128)(2,1)S(1)} %collective-permute-done.5.refs_2_.refs_11_), channel_id=1, source_target_pairs={{0,2},{1,3},{2,0},{3,1},{4,6},{5,7},{6,4},{7,5},{8,10},{9,11},{10,... | collective-permute-start | bytes 454664 | tf_op jit(solution)/shard_map/ppermute | solution.py:119
  13.2 0.0 collective-permute-done.refs_1_
  13.2 0.1 collective-permute-start.1
  13.2 0.0 collective-permute-done.2.refs_3_
  13.2 0.4 %collective-permute-start.3 = (bf16[592,128]{1,0:T(8,128)(2,1)S(1)}, bf16[592,128]{1,0:T(8,128)(2,1)S(1)}, u32[]{:S(2)}, u32[]{:S(2)}) collective-permute-start(bf16[592,128]{1,0:T(8,128)(2,1)S(1)} %collective-permute-done.2.refs_3_), channel_id=1, source_target_pairs={{0,2},{1,3},{2,0},{3,1},{4,6},{5,7},{6,4},{7,5},{8,10},{9,11},{10,... | collective-permute-start | bytes 454664 | tf_op jit(solution)/shard_map/ppermute | solution.py:119
  13.7 0.0 collective-permute-done.8.refs_5_.refs_6_
  13.7 1.5 %collective-permute-start.9 = (bf16[440,128]{1,0:T(8,128)(2,1)S(1)}, bf16[440,128]{1,0:T(8,128)(2,1)S(1)}, u32[]{:S(2)}, u32[]{:S(2)}) collective-permute-start(bf16[440,128]{1,0:T(8,128)(2,1)S(1)} %collective-permute-done.7.refs_4_.refs_0_), channel_id=1, source_target_pairs={{0,8},{1,9},{2,10},{3,11},{4,12},{5,13},{6,14},{7,15},{8,0},{9,1},... | collective-permute-start | bytes 337928 | tf_op jit(solution)/shard_map/ppermute | solution.py:119
  15.2 0.0 collective-permute-done.4.refs_1_.refs_10_
  15.2 0.0 collective-permute-done.6.refs_3_.refs_12_
  15.2 0.9 %products.3 = (f32[144,128]{1,0:T(8,128)S(1)}, f32[144,128]{1,0:T(8,128)S(1)}, f32[144,128]{1,0:T(8,128)S(1)}) custom-call(bf16[592,128]{1,0:T(8,128)(2,1)S(1)} %stacked.1.refs_0_.refs_9_, bf16[592,128]{1,0:T(8,128)(2,1)S(1)} %collective-permute-done.4.refs_1_.refs_10_, bf16[592,128]{1,0:T(8,128)(2,1)S(1)} %collective-permute-done.5.refs_2_.refs_11_, ...), custom_call_target="tpu_custom_call" | custom-call | tf_op jit(solution)/shard_map/products/pallas_call | solution.py:103
  16.1 2.7 %collective-permute-done.9.refs_8_ = bf16[440,128]{1,0:T(8,128)(2,1)S(1)} collective-permute-done((bf16[440,128]{1,0:T(8,128)(2,1)S(1)}, bf16[440,128]{1,0:T(8,128)(2,1)S(1)}, u32[]{:S(2)}, u32[]{:S(2)}) %collective-permute-start.9) | collective-permute-done | bytes 112672 | tf_op jit(solution)/shard_map/ppermute | solution.py:119
  18.8 0.0 collective-permute-done.1.refs_2_
  18.8 0.0 collective-permute-done.3.refs_4_
  18.8 1.1 %products.5 = (bf16[144,128]{1,0:T(8,128)(2,1)S(1)}, bf16[144,128]{1,0:T(8,128)(2,1)S(1)}, bf16[144,128]{1,0:T(8,128)(2,1)S(1)}) custom-call(bf16[440,128]{1,0:T(8,128)(2,1)S(1)} %collective-permute-done.7.refs_4_.refs_0_, bf16[592,128]{1,0:T(8,128)(2,1)S(1)} %collective-permute-done.refs_1_, bf16[592,128]{1,0:T(8,128)(2,1)S(1)} %collective-permute-done.1.refs_2_, ...), custom_call_target="tpu_custom_call" | custom-call | tf_op jit(solution)/shard_map/products/pallas_call | solution.py:103
  19.8 4.3 %collective-permute-start.12 = (bf16[144,128]{1,0:T(8,128)(2,1)S(1)}, bf16[144,128]{1,0:T(8,128)(2,1)S(1)}, u32[]{:S(2)}, u32[]{:S(2)}) collective-permute-start(bf16[144,128]{1,0:T(8,128)(2,1)S(1)} %get-tuple-element.16), channel_id=1, source_target_pairs={{0,24},{1,25},{2,26},{3,27},{4,28},{5,29},{6,30},{7,31},{8,16},{9,... | collective-permute-start | bytes 110600 | tf_op jit(solution)/shard_map/ppermute | solution.py:119
  24.1 0.0 collective-permute-start.11
  24.1 0.6 %collective-permute-start.10 = (bf16[144,128]{1,0:T(8,128)(2,1)S(1)}, bf16[144,128]{1,0:T(8,128)(2,1)S(1)}, u32[]{:S(2)}, u32[]{:S(2)}) collective-permute-start(bf16[144,128]{1,0:T(8,128)(2,1)S(1)} %get-tuple-element.14), channel_id=1, source_target_pairs={{0,16},{1,17},{2,18},{3,19},{4,20},{5,21},{6,22},{7,23},{8,24},{9,... | collective-permute-start | bytes 110600 | tf_op jit(solution)/shard_map/ppermute | solution.py:119
  24.8 0.0 copy-start.1
  24.8 0.5 %products.4 = f32[144,128]{1,0:T(8,128)S(1)} custom-call(bf16[592,128]{1,0:T(8,128)(2,1)S(1)} %stacked.1.refs_0_.refs_9_, bf16[592,128]{1,0:T(8,128)(2,1)S(1)} %collective-permute-done.refs_1_, bf16[592,128]{1,0:T(8,128)(2,1)S(1)} %collective-permute-done.1.refs_2_, bf16[592,128]{1,0:T(8,128)(2,1)S(1)} %collective-permute-done.2.refs_3_, ...), custom_call_target="tpu_custom_call" | custom-call | tf_op jit(solution)/shard_map/products/pallas_call | solution.py:103
  25.3 0.9 %collective-permute-done.12 = bf16[144,128]{1,0:T(8,128)(2,1)S(1)} collective-permute-done((bf16[144,128]{1,0:T(8,128)(2,1)S(1)}, bf16[144,128]{1,0:T(8,128)(2,1)S(1)}, u32[]{:S(2)}, u32[]{:S(2)}) %collective-permute-start.12) | collective-permute-done | bytes 36896 | tf_op jit(solution)/shard_map/ppermute | solution.py:119
  26.2 1.9 %collective-permute-done.11 = bf16[144,128]{1,0:T(8,128)(2,1)S(1)} collective-permute-done((bf16[144,128]{1,0:T(8,128)(2,1)S(1)}, bf16[144,128]{1,0:T(8,128)(2,1)S(1)}, u32[]{:S(2)}, u32[]{:S(2)}) %collective-permute-start.11) | collective-permute-done | bytes 36896 | tf_op jit(solution)/shard_map/ppermute | solution.py:119
  28.1 0.9 %collective-permute-done.10 = bf16[144,128]{1,0:T(8,128)(2,1)S(1)} collective-permute-done((bf16[144,128]{1,0:T(8,128)(2,1)S(1)}, bf16[144,128]{1,0:T(8,128)(2,1)S(1)}, u32[]{:S(2)}, u32[]{:S(2)}) %collective-permute-start.10) | collective-permute-done | bytes 36896 | tf_op jit(solution)/shard_map/ppermute | solution.py:119
  29.0 0.0 copy-done.1
  29.0 0.7 %fusion.3 = f32[128,144]{0,1:T(8,128)} fusion(f32[144,128]{1,0:T(8,128)S(1)} %products.4, f32[128,144]{0,1:T(8,128)S(1)} %copy-done.1, bf16[144,128]{1,0:T(8,128)(2,1)S(1)} %collective-permute-done.12, bf16[144,128]{1,0:T(8,128)(2,1)S(1)} %collective-permute-done.11, bf16[144,128]{1,0:T(8,128)(2,1)S(1)} %collective-permute-done.10), kind=kLoop, calls=%fused_computation.4 | loop fusion | flops 129024 | bytes 331776 | tf_op jit(solution)/shard_map/transpose | solution.py:152
Async XLA Ops:
  0.0 5.7 %copy-start = (bf16[128,440]{0,1:T(8,128)(2,1)S(1)}, bf16[128,440]{0,1:T(8,128)(2,1)}, u32[]{:S(2)}) copy-start(bf16[128,440]{0,1:T(8,128)(2,1)} %param.3) | copy-start | bytes 337924
  1.1 11.6 %collective-permute-start.5 = (bf16[592,128]{1,0:T(8,128)(2,1)S(1)}, bf16[592,128]{1,0:T(8,128)(2,1)S(1)}, u32[]{:S(2)}, u32[]{:S(2)}) collective-permute-start(bf16[592,128]{1,0:T(8,128)(2,1)S(1)} %stacked.1.refs_0_.refs_9_), channel_id=1, source_target_pairs={{0,5},{1,4},{2,7},{3,6},{4,1},{5,0},{6,3},{7,2},{8,13},{9,12},{10,... | collective-permute-start | bytes 454664 | tf_op jit(solution)/shard_map/ppermute | solution.py:119
  5.0 8.1 %collective-permute-start = (bf16[592,128]{1,0:T(8,128)(2,1)S(1)}, bf16[592,128]{1,0:T(8,128)(2,1)S(1)}, u32[]{:S(2)}, u32[]{:S(2)}) collective-permute-start(bf16[592,128]{1,0:T(8,128)(2,1)S(1)} %stacked.1.refs_0_.refs_9_), channel_id=1, source_target_pairs={{0,4},{1,5},{2,6},{3,7},{4,0},{5,1},{6,2},{7,3},{8,12},{9,13},{10,... | collective-permute-start | bytes 454664 | tf_op jit(solution)/shard_map/ppermute | solution.py:119
  5.6 7.7 %collective-permute-start.2 = (bf16[592,128]{1,0:T(8,128)(2,1)S(1)}, bf16[592,128]{1,0:T(8,128)(2,1)S(1)}, u32[]{:S(2)}, u32[]{:S(2)}) collective-permute-start(bf16[592,128]{1,0:T(8,128)(2,1)S(1)} %stacked.1.refs_0_.refs_9_), channel_id=1, source_target_pairs={{0,1},{1,0},{2,3},{3,2},{4,5},{5,4},{6,7},{7,6},{8,9},{9,8},{10,11... | collective-permute-start | bytes 454664 | tf_op jit(solution)/shard_map/ppermute | solution.py:119
  5.7 7.0 %collective-permute-start.7 = (bf16[440,128]{1,0:T(8,128)(2,1)S(1)}, bf16[440,128]{1,0:T(8,128)(2,1)S(1)}, u32[]{:S(2)}, u32[]{:S(2)}) collective-permute-start(bf16[440,128]{1,0:T(8,128)(2,1)S(1)} %bitcast.15), channel_id=1, source_target_pairs={{0,16},{1,17},{2,18},{3,19},{4,20},{5,21},{6,22},{7,23},{8,24},{9,... | collective-permute-start | bytes 337928 | tf_op jit(solution)/shard_map/ppermute | solution.py:119
  8.7 5.0 %collective-permute-start.8 = (bf16[440,128]{1,0:T(8,128)(2,1)S(1)}, bf16[440,128]{1,0:T(8,128)(2,1)S(1)}, u32[]{:S(2)}, u32[]{:S(2)}) collective-permute-start(bf16[440,128]{1,0:T(8,128)(2,1)S(1)} %bitcast.16), channel_id=1, source_target_pairs={{0,8},{1,9},{2,10},{3,11},{4,12},{5,13},{6,14},{7,15},{8,0},{9,1},... | collective-permute-start | bytes 337928 | tf_op jit(solution)/shard_map/ppermute | solution.py:119
  12.6 2.5 %collective-permute-start.4 = (bf16[592,128]{1,0:T(8,128)(2,1)S(1)}, bf16[592,128]{1,0:T(8,128)(2,1)S(1)}, u32[]{:S(2)}, u32[]{:S(2)}) collective-permute-start(bf16[592,128]{1,0:T(8,128)(2,1)S(1)} %stacked.1.refs_0_.refs_9_), channel_id=1, source_target_pairs={{0,2},{1,3},{2,0},{3,1},{4,6},{5,7},{6,4},{7,5},{8,10},{9,11},{10,... | collective-permute-start | bytes 454664 | tf_op jit(solution)/shard_map/ppermute | solution.py:119
  12.6 2.5 %collective-permute-start.6 = (bf16[592,128]{1,0:T(8,128)(2,1)S(1)}, bf16[592,128]{1,0:T(8,128)(2,1)S(1)}, u32[]{:S(2)}, u32[]{:S(2)}) collective-permute-start(bf16[592,128]{1,0:T(8,128)(2,1)S(1)} %collective-permute-done.5.refs_2_.refs_11_), channel_id=1, source_target_pairs={{0,2},{1,3},{2,0},{3,1},{4,6},{5,7},{6,4},{7,5},{8,10},{9,11},{10,... | collective-permute-start | bytes 454664 | tf_op jit(solution)/shard_map/ppermute | solution.py:119
  13.2 5.6 %collective-permute-start.1 = (bf16[592,128]{1,0:T(8,128)(2,1)S(1)}, bf16[592,128]{1,0:T(8,128)(2,1)S(1)}, u32[]{:S(2)}, u32[]{:S(2)}) collective-permute-start(bf16[592,128]{1,0:T(8,128)(2,1)S(1)} %collective-permute-done.refs_1_), channel_id=1, source_target_pairs={{0,2},{1,3},{2,0},{3,1},{4,6},{5,7},{6,4},{7,5},{8,10},{9,11},{10,... | collective-permute-start | bytes 454664 | tf_op jit(solution)/shard_map/ppermute | solution.py:119
  13.2 5.5 %collective-permute-start.3 = (bf16[592,128]{1,0:T(8,128)(2,1)S(1)}, bf16[592,128]{1,0:T(8,128)(2,1)S(1)}, u32[]{:S(2)}, u32[]{:S(2)}) collective-permute-start(bf16[592,128]{1,0:T(8,128)(2,1)S(1)} %collective-permute-done.2.refs_3_), channel_id=1, source_target_pairs={{0,2},{1,3},{2,0},{3,1},{4,6},{5,7},{6,4},{7,5},{8,10},{9,11},{10,... | collective-permute-start | bytes 454664 | tf_op jit(solution)/shard_map/ppermute | solution.py:119
  13.7 5.1 %collective-permute-start.9 = (bf16[440,128]{1,0:T(8,128)(2,1)S(1)}, bf16[440,128]{1,0:T(8,128)(2,1)S(1)}, u32[]{:S(2)}, u32[]{:S(2)}) collective-permute-start(bf16[440,128]{1,0:T(8,128)(2,1)S(1)} %collective-permute-done.7.refs_4_.refs_0_), channel_id=1, source_target_pairs={{0,8},{1,9},{2,10},{3,11},{4,12},{5,13},{6,14},{7,15},{8,0},{9,1},... | collective-permute-start | bytes 337928 | tf_op jit(solution)/shard_map/ppermute | solution.py:119
  19.8 6.4 %collective-permute-start.12 = (bf16[144,128]{1,0:T(8,128)(2,1)S(1)}, bf16[144,128]{1,0:T(8,128)(2,1)S(1)}, u32[]{:S(2)}, u32[]{:S(2)}) collective-permute-start(bf16[144,128]{1,0:T(8,128)(2,1)S(1)} %get-tuple-element.16), channel_id=1, source_target_pairs={{0,24},{1,25},{2,26},{3,27},{4,28},{5,29},{6,30},{7,31},{8,16},{9,... | collective-permute-start | bytes 110600 | tf_op jit(solution)/shard_map/ppermute | solution.py:119
  24.1 4.0 %collective-permute-start.11 = (bf16[144,128]{1,0:T(8,128)(2,1)S(1)}, bf16[144,128]{1,0:T(8,128)(2,1)S(1)}, u32[]{:S(2)}, u32[]{:S(2)}) collective-permute-start(bf16[144,128]{1,0:T(8,128)(2,1)S(1)} %get-tuple-element.15), channel_id=1, source_target_pairs={{0,8},{1,9},{2,10},{3,11},{4,12},{5,13},{6,14},{7,15},{8,0},{9,1},... | collective-permute-start | bytes 110600 | tf_op jit(solution)/shard_map/ppermute | solution.py:119
  24.1 4.9 %collective-permute-start.10 = (bf16[144,128]{1,0:T(8,128)(2,1)S(1)}, bf16[144,128]{1,0:T(8,128)(2,1)S(1)}, u32[]{:S(2)}, u32[]{:S(2)}) collective-permute-start(bf16[144,128]{1,0:T(8,128)(2,1)S(1)} %get-tuple-element.14), channel_id=1, source_target_pairs={{0,16},{1,17},{2,18},{3,19},{4,20},{5,21},{6,22},{7,23},{8,24},{9,... | collective-permute-start | bytes 110600 | tf_op jit(solution)/shard_map/ppermute | solution.py:119
  24.8 4.2 %copy-start.1 = (f32[128,144]{0,1:T(8,128)S(1)}, f32[128,144]{0,1:T(8,128)}, u32[]{:S(2)}) copy-start(f32[128,144]{0,1:T(8,128)} %param.5) | copy-start | bytes 221188
where the time goes:
time: 29.8 us; the launch traced here: 29.7 us
  starting transfers between devices  16.7 us (56%)
  waiting for transfers between devices  8.81 us (30%)
  Pallas kernels  3.5 us (12%)
  other arithmetic  0.66 us (2%)
    ppermute x13, starting transfers between devices, swap(): return lax.ppermute(value, AXES, [(i, i ^ bits) for i in range(total)])  16.7 us
    ppermute x13, waiting for transfers between devices, swap(): return lax.ppermute(value, AXES, [(i, i ^ bits) for i in range(total)])  8.81 us
    pallas_call x3, Pallas kernels, products(): pl.pallas_call(body, out_shape=shapes, in_specs=[vmem] * count, out_specs...  2.44 us
    pallas_call x1, Pallas kernels, stacked(): pl.pallas_call(body, out_shape=pltpu.VMEM(shape, values.dtype) if near el...  1.05 us
    transpose x1, other arithmetic, per_device(): return result.T  0.66 us
  transfers between devices with their start and end apart: 13, of which 5 were waited for; matrix products, arithmetic and copies ran while one was open for 0% of the time, Pallas kernels for 5%

commit v1 on v0

--- a/solution.py
+++ b/solution.py
@@ -70,7 +70,7 @@
             left_ref[n, :feats, :] = (wide * -2.0).astype(jnp.bfloat16)
             left_ref[n, feats:, :] = square_rows(wide, 3)
         lhs = [left_ref[n].T for n in range(len(plan))]
-        acc = [None if old is None else ins[old][...] for _, _, old in plan]
+        acc = [None for _ in plan]
         groups = []
         for _, keys, _ in plan:
             for n in range(0, len(keys), 2):
@@ -85,13 +85,16 @@
             d2 = jnp.maximum(jnp.dot(left, rhs, preferred_element_type=jnp.float32), 1e-30)
             kern = jnp.exp2((d2 * -LOG2E) * lax.rsqrt(d2)).astype(jnp.bfloat16)
             part = lax.dot_general(
-                weight, kern, (((1,), (1,)), ((), ())), preferred_element_type=jnp.float32
+                kern, weight, (((1,), (1,)), ((), ())), preferred_element_type=jnp.float32
             )
             for n, i in enumerate(users):
-                mine = part[:, n * width:(n + 1) * width]
+                mine = part[n * width:(n + 1) * width, :]
                 acc[i] = mine if acc[i] is None else acc[i] + mine
         for i in range(len(plan)):
-            out_refs[i][...] = acc[i].astype(out_refs[i].dtype)
+            total = acc[i].T
+            old = plan[i][2]
+            total = total if old is None else total + ins[old][...]
+            out_refs[i][...] = total.astype(out_refs[i].dtype)
 
     shapes = [((outs, width), kind) for kind in kinds]
     vmem = pl.BlockSpec(memory_space=pltpu.VMEM)

time: 29.8 us -> 29.7 us (level)
  transfers between devices with their start and end apart: 13 -> 13, of which waited for: 5 -> 5; matrix products, arithmetic and copies ran while one was open for 0% -> 0% of each run, Pallas kernels for 5% -> 4%
where the time goes in v1:
time: 29.7 us; the launch traced here: 29.6 us
  starting transfers between devices  16.7 us (56%)
  waiting for transfers between devices  8.89 us (30%)
  Pallas kernels  3.36 us (11%)
  other arithmetic  0.66 us (2%)
    ppermute x13, starting transfers between devices, swap(): return lax.ppermute(value, AXES, [(i, i ^ bits) for i in range(total)])  16.7 us
    ppermute x13, waiting for transfers between devices, swap(): return lax.ppermute(value, AXES, [(i, i ^ bits) for i in range(total)])  8.89 us
    pallas_call x3, Pallas kernels, products(): pl.pallas_call(body, out_shape=shapes, in_specs=[vmem] * count, out_specs...  2.3 us
    pallas_call x1, Pallas kernels, stacked(): pl.pallas_call(body, out_shape=pltpu.VMEM(shape, values.dtype) if near el...  1.05 us
    transpose x1, other arithmetic, per_device(): return result.T  0.66 us
  transfers between devices with their start and end apart: 13, of which 5 were waited for; matrix products, arithmetic and copies ran while one was open for 0% of the time, Pallas kernels for 4%

profile of v1, /device:TPU:0, one launch (start us, length us, event | category | flops | bytes accessed | tf_op | source)
XLA Modules:
  0.0 29.6 jit_solution(6787848363467885451)
XLA Ops:
  0.0 0.0 copy-start
  0.0 1.1 %stacked.1.refs_0_.refs_9_ = bf16[592,128]{1,0:T(8,128)(2,1)S(1)} custom-call(bf16[144,128]{1,0:T(8,128)(2,1)} %bitcast.17, bf16[440,128]{1,0:T(8,128)(2,1)} %bitcast.14), custom_call_target="tpu_custom_call" | custom-call | tf_op jit(solution)/shard_map/stacked/pallas_call | solution.py:39
  1.1 4.0 %collective-permute-start.5 = (bf16[592,128]{1,0:T(8,128)(2,1)S(1)}, bf16[592,128]{1,0:T(8,128)(2,1)S(1)}, u32[]{:S(2)}, u32[]{:S(2)}) collective-permute-start(bf16[592,128]{1,0:T(8,128)(2,1)S(1)} %stacked.1.refs_0_.refs_9_), channel_id=1, source_target_pairs={{0,5},{1,4},{2,7},{3,6},{4,1},{5,0},{6,3},{7,2},{8,13},{9,12},{10,... | collective-permute-start | bytes 454664 | tf_op jit(solution)/shard_map/ppermute | solution.py:122
  5.0 0.5 %collective-permute-start = (bf16[592,128]{1,0:T(8,128)(2,1)S(1)}, bf16[592,128]{1,0:T(8,128)(2,1)S(1)}, u32[]{:S(2)}, u32[]{:S(2)}) collective-permute-start(bf16[592,128]{1,0:T(8,128)(2,1)S(1)} %stacked.1.refs_0_.refs_9_), channel_id=1, source_target_pairs={{0,4},{1,5},{2,6},{3,7},{4,0},{5,1},{6,2},{7,3},{8,12},{9,13},{10,... | collective-permute-start | bytes 454664 | tf_op jit(solution)/shard_map/ppermute | solution.py:122
  5.6 0.1 collective-permute-start.2
  5.7 0.0 copy-done
  5.7 3.0 %collective-permute-start.7 = (bf16[440,128]{1,0:T(8,128)(2,1)S(1)}, bf16[440,128]{1,0:T(8,128)(2,1)S(1)}, u32[]{:S(2)}, u32[]{:S(2)}) collective-permute-start(bf16[440,128]{1,0:T(8,128)(2,1)S(1)} %bitcast.15), channel_id=1, source_target_pairs={{0,16},{1,17},{2,18},{3,19},{4,20},{5,21},{6,22},{7,23},{8,24},{9,... | collective-permute-start | bytes 337928 | tf_op jit(solution)/shard_map/ppermute | solution.py:122
  8.7 1.6 %collective-permute-start.8 = (bf16[440,128]{1,0:T(8,128)(2,1)S(1)}, bf16[440,128]{1,0:T(8,128)(2,1)S(1)}, u32[]{:S(2)}, u32[]{:S(2)}) collective-permute-start(bf16[440,128]{1,0:T(8,128)(2,1)S(1)} %bitcast.16), channel_id=1, source_target_pairs={{0,8},{1,9},{2,10},{3,11},{4,12},{5,13},{6,14},{7,15},{8,0},{9,1},... | collective-permute-start | bytes 337928 | tf_op jit(solution)/shard_map/ppermute | solution.py:122
  10.2 2.4 %collective-permute-done.7.refs_4_.refs_0_ = bf16[440,128]{1,0:T(8,128)(2,1)S(1)} collective-permute-done((bf16[440,128]{1,0:T(8,128)(2,1)S(1)}, bf16[440,128]{1,0:T(8,128)(2,1)S(1)}, u32[]{:S(2)}, u32[]{:S(2)}) %collective-permute-start.7) | collective-permute-done | bytes 112672 | tf_op jit(solution)/shard_map/ppermute | solution.py:122
  12.6 0.0 collective-permute-start.4
  12.6 0.0 collective-permute-done.5.refs_2_.refs_11_
  12.6 0.5 %collective-permute-start.6 = (bf16[592,128]{1,0:T(8,128)(2,1)S(1)}, bf16[592,128]{1,0:T(8,128)(2,1)S(1)}, u32[]{:S(2)}, u32[]{:S(2)}) collective-permute-start(bf16[592,128]{1,0:T(8,128)(2,1)S(1)} %collective-permute-done.5.refs_2_.refs_11_), channel_id=1, source_target_pairs={{0,2},{1,3},{2,0},{3,1},{4,6},{5,7},{6,4},{7,5},{8,10},{9,11},{10,... | collective-permute-start | bytes 454664 | tf_op jit(solution)/shard_map/ppermute | solution.py:122
  13.2 0.0 collective-permute-done.refs_1_
  13.2 0.1 collective-permute-start.1
  13.2 0.0 collective-permute-done.2.refs_3_
  13.2 0.4 %collective-permute-start.3 = (bf16[592,128]{1,0:T(8,128)(2,1)S(1)}, bf16[592,128]{1,0:T(8,128)(2,1)S(1)}, u32[]{:S(2)}, u32[]{:S(2)}) collective-permute-start(bf16[592,128]{1,0:T(8,128)(2,1)S(1)} %collective-permute-done.2.refs_3_), channel_id=1, source_target_pairs={{0,2},{1,3},{2,0},{3,1},{4,6},{5,7},{6,4},{7,5},{8,10},{9,11},{10,... | collective-permute-start | bytes 454664 | tf_op jit(solution)/shard_map/ppermute | solution.py:122
  13.7 0.0 collective-permute-done.8.refs_5_.refs_6_
  13.7 1.5 %collective-permute-start.9 = (bf16[440,128]{1,0:T(8,128)(2,1)S(1)}, bf16[440,128]{1,0:T(8,128)(2,1)S(1)}, u32[]{:S(2)}, u32[]{:S(2)}) collective-permute-start(bf16[440,128]{1,0:T(8,128)(2,1)S(1)} %collective-permute-done.7.refs_4_.refs_0_), channel_id=1, source_target_pairs={{0,8},{1,9},{2,10},{3,11},{4,12},{5,13},{6,14},{7,15},{8,0},{9,1},... | collective-permute-start | bytes 337928 | tf_op jit(solution)/shard_map/ppermute | solution.py:122
  15.2 0.0 collective-permute-done.4.refs_1_.refs_10_
  15.2 0.0 collective-permute-done.6.refs_3_.refs_12_
  15.2 0.8 %products.3 = (f32[144,128]{1,0:T(8,128)S(1)}, f32[144,128]{1,0:T(8,128)S(1)}, f32[144,128]{1,0:T(8,128)S(1)}) custom-call(bf16[592,128]{1,0:T(8,128)(2,1)S(1)} %stacked.1.refs_0_.refs_9_, bf16[592,128]{1,0:T(8,128)(2,1)S(1)} %collective-permute-done.4.refs_1_.refs_10_, bf16[592,128]{1,0:T(8,128)(2,1)S(1)} %collective-permute-done.5.refs_2_.refs_11_, ...), custom_call_target="tpu_custom_call" | custom-call | tf_op jit(solution)/shard_map/products/pallas_call | solution.py:106
  15.9 2.8 %collective-permute-done.9.refs_8_ = bf16[440,128]{1,0:T(8,128)(2,1)S(1)} collective-permute-done((bf16[440,128]{1,0:T(8,128)(2,1)S(1)}, bf16[440,128]{1,0:T(8,128)(2,1)S(1)}, u32[]{:S(2)}, u32[]{:S(2)}) %collective-permute-start.9) | collective-permute-done | bytes 112672 | tf_op jit(solution)/shard_map/ppermute | solution.py:122
  18.8 0.0 collective-permute-done.1.refs_2_
  18.8 0.0 collective-permute-done.3.refs_4_
  18.8 1.0 %products.5 = (bf16[144,128]{1,0:T(8,128)(2,1)S(1)}, bf16[144,128]{1,0:T(8,128)(2,1)S(1)}, bf16[144,128]{1,0:T(8,128)(2,1)S(1)}) custom-call(bf16[440,128]{1,0:T(8,128)(2,1)S(1)} %collective-permute-done.7.refs_4_.refs_0_, bf16[592,128]{1,0:T(8,128)(2,1)S(1)} %collective-permute-done.refs_1_, bf16[592,128]{1,0:T(8,128)(2,1)S(1)} %collective-permute-done.1.refs_2_, ...), custom_call_target="tpu_custom_call" | custom-call | tf_op jit(solution)/shard_map/products/pallas_call | solution.py:106
  19.8 4.3 %collective-permute-start.12 = (bf16[144,128]{1,0:T(8,128)(2,1)S(1)}, bf16[144,128]{1,0:T(8,128)(2,1)S(1)}, u32[]{:S(2)}, u32[]{:S(2)}) collective-permute-start(bf16[144,128]{1,0:T(8,128)(2,1)S(1)} %get-tuple-element.16), channel_id=1, source_target_pairs={{0,24},{1,25},{2,26},{3,27},{4,28},{5,29},{6,30},{7,31},{8,16},{9,... | collective-permute-start | bytes 110600 | tf_op jit(solution)/shard_map/ppermute | solution.py:122
  24.1 0.0 collective-permute-start.11
  24.1 0.6 %collective-permute-start.10 = (bf16[144,128]{1,0:T(8,128)(2,1)S(1)}, bf16[144,128]{1,0:T(8,128)(2,1)S(1)}, u32[]{:S(2)}, u32[]{:S(2)}) collective-permute-start(bf16[144,128]{1,0:T(8,128)(2,1)S(1)} %get-tuple-element.14), channel_id=1, source_target_pairs={{0,16},{1,17},{2,18},{3,19},{4,20},{5,21},{6,22},{7,23},{8,24},{9,... | collective-permute-start | bytes 110600 | tf_op jit(solution)/shard_map/ppermute | solution.py:122
  24.7 0.0 copy-start.1
  24.7 0.6 %products.4 = f32[144,128]{1,0:T(8,128)S(1)} custom-call(bf16[592,128]{1,0:T(8,128)(2,1)S(1)} %stacked.1.refs_0_.refs_9_, bf16[592,128]{1,0:T(8,128)(2,1)S(1)} %collective-permute-done.refs_1_, bf16[592,128]{1,0:T(8,128)(2,1)S(1)} %collective-permute-done.1.refs_2_, bf16[592,128]{1,0:T(8,128)(2,1)S(1)} %collective-permute-done.2.refs_3_, ...), custom_call_target="tpu_custom_call" | custom-call | tf_op jit(solution)/shard_map/products/pallas_call | solution.py:106
  25.3 0.8 %collective-permute-done.12 = bf16[144,128]{1,0:T(8,128)(2,1)S(1)} collective-permute-done((bf16[144,128]{1,0:T(8,128)(2,1)S(1)}, bf16[144,128]{1,0:T(8,128)(2,1)S(1)}, u32[]{:S(2)}, u32[]{:S(2)}) %collective-permute-start.12) | collective-permute-done | bytes 36896 | tf_op jit(solution)/shard_map/ppermute | solution.py:122
  26.1 1.9 %collective-permute-done.11 = bf16[144,128]{1,0:T(8,128)(2,1)S(1)} collective-permute-done((bf16[144,128]{1,0:T(8,128)(2,1)S(1)}, bf16[144,128]{1,0:T(8,128)(2,1)S(1)}, u32[]{:S(2)}, u32[]{:S(2)}) %collective-permute-start.11) | collective-permute-done | bytes 36896 | tf_op jit(solution)/shard_map/ppermute | solution.py:122
  28.0 0.9 %collective-permute-done.10 = bf16[144,128]{1,0:T(8,128)(2,1)S(1)} collective-permute-done((bf16[144,128]{1,0:T(8,128)(2,1)S(1)}, bf16[144,128]{1,0:T(8,128)(2,1)S(1)}, u32[]{:S(2)}, u32[]{:S(2)}) %collective-permute-start.10) | collective-permute-done | bytes 36896 | tf_op jit(solution)/shard_map/ppermute | solution.py:122
  28.9 0.0 copy-done.1
  28.9 0.7 %fusion.3 = f32[128,144]{0,1:T(8,128)} fusion(f32[144,128]{1,0:T(8,128)S(1)} %products.4, f32[128,144]{0,1:T(8,128)S(1)} %copy-done.1, bf16[144,128]{1,0:T(8,128)(2,1)S(1)} %collective-permute-done.12, bf16[144,128]{1,0:T(8,128)(2,1)S(1)} %collective-permute-done.11, bf16[144,128]{1,0:T(8,128)(2,1)S(1)} %collective-permute-done.10), kind=kLoop, calls=%fused_computation.4 | loop fusion | flops 129024 | bytes 331776 | tf_op jit(solution)/shard_map/transpose | solution.py:155
Async XLA Ops:
  0.0 5.7 %copy-start = (bf16[128,440]{0,1:T(8,128)(2,1)S(1)}, bf16[128,440]{0,1:T(8,128)(2,1)}, u32[]{:S(2)}) copy-start(bf16[128,440]{0,1:T(8,128)(2,1)} %param.3) | copy-start | bytes 337924
  1.1 11.6 %collective-permute-start.5 = (bf16[592,128]{1,0:T(8,128)(2,1)S(1)}, bf16[592,128]{1,0:T(8,128)(2,1)S(1)}, u32[]{:S(2)}, u32[]{:S(2)}) collective-permute-start(bf16[592,128]{1,0:T(8,128)(2,1)S(1)} %stacked.1.refs_0_.refs_9_), channel_id=1, source_target_pairs={{0,5},{1,4},{2,7},{3,6},{4,1},{5,0},{6,3},{7,2},{8,13},{9,12},{10,... | collective-permute-start | bytes 454664 | tf_op jit(solution)/shard_map/ppermute | solution.py:122
  5.0 8.1 %collective-permute-start = (bf16[592,128]{1,0:T(8,128)(2,1)S(1)}, bf16[592,128]{1,0:T(8,128)(2,1)S(1)}, u32[]{:S(2)}, u32[]{:S(2)}) collective-permute-start(bf16[592,128]{1,0:T(8,128)(2,1)S(1)} %stacked.1.refs_0_.refs_9_), channel_id=1, source_target_pairs={{0,4},{1,5},{2,6},{3,7},{4,0},{5,1},{6,2},{7,3},{8,12},{9,13},{10,... | collective-permute-start | bytes 454664 | tf_op jit(solution)/shard_map/ppermute | solution.py:122
  5.6 7.7 %collective-permute-start.2 = (bf16[592,128]{1,0:T(8,128)(2,1)S(1)}, bf16[592,128]{1,0:T(8,128)(2,1)S(1)}, u32[]{:S(2)}, u32[]{:S(2)}) collective-permute-start(bf16[592,128]{1,0:T(8,128)(2,1)S(1)} %stacked.1.refs_0_.refs_9_), channel_id=1, source_target_pairs={{0,1},{1,0},{2,3},{3,2},{4,5},{5,4},{6,7},{7,6},{8,9},{9,8},{10,11... | collective-permute-start | bytes 454664 | tf_op jit(solution)/shard_map/ppermute | solution.py:122
  5.7 7.0 %collective-permute-start.7 = (bf16[440,128]{1,0:T(8,128)(2,1)S(1)}, bf16[440,128]{1,0:T(8,128)(2,1)S(1)}, u32[]{:S(2)}, u32[]{:S(2)}) collective-permute-start(bf16[440,128]{1,0:T(8,128)(2,1)S(1)} %bitcast.15), channel_id=1, source_target_pairs={{0,16},{1,17},{2,18},{3,19},{4,20},{5,21},{6,22},{7,23},{8,24},{9,... | collective-permute-start | bytes 337928 | tf_op jit(solution)/shard_map/ppermute | solution.py:122
  8.7 5.0 %collective-permute-start.8 = (bf16[440,128]{1,0:T(8,128)(2,1)S(1)}, bf16[440,128]{1,0:T(8,128)(2,1)S(1)}, u32[]{:S(2)}, u32[]{:S(2)}) collective-permute-start(bf16[440,128]{1,0:T(8,128)(2,1)S(1)} %bitcast.16), channel_id=1, source_target_pairs={{0,8},{1,9},{2,10},{3,11},{4,12},{5,13},{6,14},{7,15},{8,0},{9,1},... | collective-permute-start | bytes 337928 | tf_op jit(solution)/shard_map/ppermute | solution.py:122
  12.6 2.5 %collective-permute-start.4 = (bf16[592,128]{1,0:T(8,128)(2,1)S(1)}, bf16[592,128]{1,0:T(8,128)(2,1)S(1)}, u32[]{:S(2)}, u32[]{:S(2)}) collective-permute-start(bf16[592,128]{1,0:T(8,128)(2,1)S(1)} %stacked.1.refs_0_.refs_9_), channel_id=1, source_target_pairs={{0,2},{1,3},{2,0},{3,1},{4,6},{5,7},{6,4},{7,5},{8,10},{9,11},{10,... | collective-permute-start | bytes 454664 | tf_op jit(solution)/shard_map/ppermute | solution.py:122
  12.6 2.5 %collective-permute-start.6 = (bf16[592,128]{1,0:T(8,128)(2,1)S(1)}, bf16[592,128]{1,0:T(8,128)(2,1)S(1)}, u32[]{:S(2)}, u32[]{:S(2)}) collective-permute-start(bf16[592,128]{1,0:T(8,128)(2,1)S(1)} %collective-permute-done.5.refs_2_.refs_11_), channel_id=1, source_target_pairs={{0,2},{1,3},{2,0},{3,1},{4,6},{5,7},{6,4},{7,5},{8,10},{9,11},{10,... | collective-permute-start | bytes 454664 | tf_op jit(solution)/shard_map/ppermute | solution.py:122
  13.2 5.6 %collective-permute-start.1 = (bf16[592,128]{1,0:T(8,128)(2,1)S(1)}, bf16[592,128]{1,0:T(8,128)(2,1)S(1)}, u32[]{:S(2)}, u32[]{:S(2)}) collective-permute-start(bf16[592,128]{1,0:T(8,128)(2,1)S(1)} %collective-permute-done.refs_1_), channel_id=1, source_target_pairs={{0,2},{1,3},{2,0},{3,1},{4,6},{5,7},{6,4},{7,5},{8,10},{9,11},{10,... | collective-permute-start | bytes 454664 | tf_op jit(solution)/shard_map/ppermute | solution.py:122
  13.2 5.5 %collective-permute-start.3 = (bf16[592,128]{1,0:T(8,128)(2,1)S(1)}, bf16[592,128]{1,0:T(8,128)(2,1)S(1)}, u32[]{:S(2)}, u32[]{:S(2)}) collective-permute-start(bf16[592,128]{1,0:T(8,128)(2,1)S(1)} %collective-permute-done.2.refs_3_), channel_id=1, source_target_pairs={{0,2},{1,3},{2,0},{3,1},{4,6},{5,7},{6,4},{7,5},{8,10},{9,11},{10,... | collective-permute-start | bytes 454664 | tf_op jit(solution)/shard_map/ppermute | solution.py:122
  13.7 5.1 %collective-permute-start.9 = (bf16[440,128]{1,0:T(8,128)(2,1)S(1)}, bf16[440,128]{1,0:T(8,128)(2,1)S(1)}, u32[]{:S(2)}, u32[]{:S(2)}) collective-permute-start(bf16[440,128]{1,0:T(8,128)(2,1)S(1)} %collective-permute-done.7.refs_4_.refs_0_), channel_id=1, source_target_pairs={{0,8},{1,9},{2,10},{3,11},{4,12},{5,13},{6,14},{7,15},{8,0},{9,1},... | collective-permute-start | bytes 337928 | tf_op jit(solution)/shard_map/ppermute | solution.py:122
  19.8 6.4 %collective-permute-start.12 = (bf16[144,128]{1,0:T(8,128)(2,1)S(1)}, bf16[144,128]{1,0:T(8,128)(2,1)S(1)}, u32[]{:S(2)}, u32[]{:S(2)}) collective-permute-start(bf16[144,128]{1,0:T(8,128)(2,1)S(1)} %get-tuple-element.16), channel_id=1, source_target_pairs={{0,24},{1,25},{2,26},{3,27},{4,28},{5,29},{6,30},{7,31},{8,16},{9,... | collective-permute-start | bytes 110600 | tf_op jit(solution)/shard_map/ppermute | solution.py:122
  24.1 4.0 %collective-permute-start.11 = (bf16[144,128]{1,0:T(8,128)(2,1)S(1)}, bf16[144,128]{1,0:T(8,128)(2,1)S(1)}, u32[]{:S(2)}, u32[]{:S(2)}) collective-permute-start(bf16[144,128]{1,0:T(8,128)(2,1)S(1)} %get-tuple-element.15), channel_id=1, source_target_pairs={{0,8},{1,9},{2,10},{3,11},{4,12},{5,13},{6,14},{7,15},{8,0},{9,1},... | collective-permute-start | bytes 110600 | tf_op jit(solution)/shard_map/ppermute | solution.py:122
  24.1 4.9 %collective-permute-start.10 = (bf16[144,128]{1,0:T(8,128)(2,1)S(1)}, bf16[144,128]{1,0:T(8,128)(2,1)S(1)}, u32[]{:S(2)}, u32[]{:S(2)}) collective-permute-start(bf16[144,128]{1,0:T(8,128)(2,1)S(1)} %get-tuple-element.14), channel_id=1, source_target_pairs={{0,16},{1,17},{2,18},{3,19},{4,20},{5,21},{6,22},{7,23},{8,24},{9,... | collective-permute-start | bytes 110600 | tf_op jit(solution)/shard_map/ppermute | solution.py:122
  24.7 4.2 %copy-start.1 = (f32[128,144]{0,1:T(8,128)S(1)}, f32[128,144]{0,1:T(8,128)}, u32[]{:S(2)}) copy-start(f32[128,144]{0,1:T(8,128)} %param.5) | copy-start | bytes 221188

commit v2 on v1

--- a/solution.py
+++ b/solution.py
@@ -45,7 +45,7 @@
     )(weights, values)
 
 
-def products(work, outs, feats, kinds, near):
+def products(work, outs, feats, kinds, near, prepared=0):
     arrays, slots = [], {}
 
     def slot(a):
@@ -55,24 +55,34 @@
         return slots[id(a)]
 
     plan = [
-        (slot(q), [slot(k) for k in keys], None if old is None else slot(old))
+        (
+            slot(q[0] if isinstance(q, tuple) else q),
+            isinstance(q, tuple),
+            [slot(k) for k in keys],
+            None if old is None else slot(old),
+        )
         for q, keys, old in work
     ]
-    count = len(arrays)
-    width = work[0][0].shape[1]
+    count, entries = len(arrays), len(work)
+    width = work[0][1][0].shape[1]
 
     def body(*refs):
         ins, out_refs, left_ref = refs[:count], refs[count:-1], refs[-1]
-        for n, (q, _, _) in enumerate(plan):
+        lhs = []
+        for n, (q, ready, _, _) in enumerate(plan):
+            if ready:
+                lhs.append(ins[q][...])
+                continue
             skip = outs if ins[q].shape[0] > feats else 0
-            value = ins[q][skip:skip + feats, :]
-            wide = value.astype(jnp.float32)
+            wide = ins[q][skip:skip + feats, :].astype(jnp.float32)
             left_ref[n, :feats, :] = (wide * -2.0).astype(jnp.bfloat16)
             left_ref[n, feats:, :] = square_rows(wide, 3)
-        lhs = [left_ref[n].T for n in range(len(plan))]
+            lhs.append(left_ref[n].T)
+        for n in range(prepared):
+            out_refs[entries + n][...] = lhs[entries - prepared + n]
         acc = [None for _ in plan]
         groups = []
-        for _, keys, _ in plan:
+        for _, _, keys, _ in plan:
             for n in range(0, len(keys), 2):
                 group = tuple(keys[n:n + 2])
                 if group not in groups:
@@ -80,7 +90,7 @@
         for group in groups:
             rhs = jnp.concatenate([ins[k][outs:, :] for k in group], axis=1)
             weight = jnp.concatenate([ins[k][:outs, :] for k in group], axis=1)
-            users = [i for i, (_, keys, _) in enumerate(plan) if group[0] in keys]
+            users = [i for i, (_, _, keys, _) in enumerate(plan) if group[0] in keys]
             left = jnp.concatenate([lhs[i] for i in users], axis=0)
             d2 = jnp.maximum(jnp.dot(left, rhs, preferred_element_type=jnp.float32), 1e-30)
             kern = jnp.exp2((d2 * -LOG2E) * lax.rsqrt(d2)).astype(jnp.bfloat16)
@@ -90,13 +100,14 @@
             for n, i in enumerate(users):
                 mine = part[n * width:(n + 1) * width, :]
                 acc[i] = mine if acc[i] is None else acc[i] + mine
-        for i in range(len(plan)):
+        for i in range(entries):
             total = acc[i].T
-            old = plan[i][2]
+            old = plan[i][3]
             total = total if old is None else total + ins[old][...]
             out_refs[i][...] = total.astype(out_refs[i].dtype)
 
     shapes = [((outs, width), kind) for kind in kinds]
+    shapes = shapes + [((width, feats + 8), jnp.bfloat16)] * prepared
     vmem = pl.BlockSpec(memory_space=pltpu.VMEM)
     if near:
         arrays = [pltpu.with_memory_space_constraint(a, pltpu.VMEM) for a in arrays]
@@ -107,8 +118,8 @@
         body,
         out_shape=shapes,
         in_specs=[vmem] * count,
-        out_specs=[vmem] * len(work),
-        scratch_shapes=[pltpu.VMEM((len(work), feats + 8, width), jnp.bfloat16)],
+        out_specs=[vmem] * len(shapes),
+        scratch_shapes=[pltpu.VMEM((entries, feats + 8, width), jnp.bfloat16)],
         name="products",
     )(*arrays)
 
@@ -144,11 +155,13 @@
     feats = mine.shape[0]
     half = len(keys) // 2
     lead = queries[:-1] if len(queries) > 1 else queries
-    early = products([(q, keys[:half], None) for q in lead], outs, feats, [f32] * len(lead), near)
-    sent = [(q, keys[half:], e) for q, e in zip(lead, early)][1:]
+    run = functools.partial(products, outs=outs, feats=feats, near=near)
+    got = run([(q, keys[:half], None) for q in lead], kinds=[f32] * len(lead), prepared=len(lead))
+    early, ready = got[:len(lead)], [(a,) for a in got[len(lead):]]
+    sent = [(q, keys[half:], e) for q, e in zip(ready, early)][1:]
     sent = sent + [(q, keys, None) for q in queries[len(lead):]]
-    parts = products(sent, outs, feats, [b16] * len(sent), near) if sent else []
-    own = products([(queries[0], keys[half:], early[0])], outs, feats, [f32], near)[0]
+    parts = run(sent, kinds=[b16] * len(sent)) if sent else []
+    own = run([(ready[0], keys[half:], early[0])], kinds=[f32])[0]
     result = own - targets.T
     for n, part in enumerate(parts):
         result = result + swap(part, order[n + 1]).astype(f32)

time: 29.7 us -> 29.7 us (level)
  no operation moved by 1% of the time
where the time goes in v2:
time: 29.7 us; the launch traced here: 29.5 us
  starting transfers between devices  16.7 us (56%)
  waiting for transfers between devices  8.93 us (30%)
  Pallas kernels  3.26 us (11%)
  other arithmetic  0.66 us (2%)
    ppermute x13, starting transfers between devices, swap(): return lax.ppermute(value, AXES, [(i, i ^ bits) for i in range(total)])  16.7 us
    ppermute x13, waiting for transfers between devices, swap(): return lax.ppermute(value, AXES, [(i, i ^ bits) for i in range(total)])  8.93 us
    pallas_call x3, Pallas kernels, products(): pl.pallas_call(body, out_shape=shapes, in_specs=[vmem] * count, out_specs...  2.21 us
    pallas_call x1, Pallas kernels, stacked(): pl.pallas_call(body, out_shape=pltpu.VMEM(shape, values.dtype) if near el...  1.05 us
    transpose x1, other arithmetic, per_device(): return result.T  0.66 us
  transfers between devices with their start and end apart: 13, of which 5 were waited for; matrix products, arithmetic and copies ran while one was open for 0% of the time, Pallas kernels for 4%

profile of v2, /device:TPU:0, one launch (start us, length us, event | category | flops | bytes accessed | tf_op | source)
XLA Modules:
  0.0 29.5 jit_solution(8010677820859543544)
XLA Ops:
  0.0 0.0 copy-start
  0.0 1.1 %stacked.1.refs_0_.refs_9_ = bf16[592,128]{1,0:T(8,128)(2,1)S(1)} custom-call(bf16[144,128]{1,0:T(8,128)(2,1)} %bitcast.17, bf16[440,128]{1,0:T(8,128)(2,1)} %bitcast.14), custom_call_target="tpu_custom_call" | custom-call | tf_op jit(solution)/shard_map/stacked/pallas_call | solution.py:39
  1.1 4.0 %collective-permute-start.1 = (bf16[592,128]{1,0:T(8,128)(2,1)S(1)}, bf16[592,128]{1,0:T(8,128)(2,1)S(1)}, u32[]{:S(2)}, u32[]{:S(2)}) collective-permute-start(bf16[592,128]{1,0:T(8,128)(2,1)S(1)} %stacked.1.refs_0_.refs_9_), channel_id=1, source_target_pairs={{0,5},{1,4},{2,7},{3,6},{4,1},{5,0},{6,3},{7,2},{8,13},{9,12},{10,... | collective-permute-start | bytes 454664 | tf_op jit(solution)/shard_map/ppermute | solution.py:133
  5.0 0.5 %collective-permute-start.5 = (bf16[592,128]{1,0:T(8,128)(2,1)S(1)}, bf16[592,128]{1,0:T(8,128)(2,1)S(1)}, u32[]{:S(2)}, u32[]{:S(2)}) collective-permute-start(bf16[592,128]{1,0:T(8,128)(2,1)S(1)} %stacked.1.refs_0_.refs_9_), channel_id=1, source_target_pairs={{0,4},{1,5},{2,6},{3,7},{4,0},{5,1},{6,2},{7,3},{8,12},{9,13},{10,... | collective-permute-start | bytes 454664 | tf_op jit(solution)/shard_map/ppermute | solution.py:133
  5.6 0.1 collective-permute-start.7
  5.7 0.0 copy-done
  5.7 3.0 %collective-permute-start.3 = (bf16[440,128]{1,0:T(8,128)(2,1)S(1)}, bf16[440,128]{1,0:T(8,128)(2,1)S(1)}, u32[]{:S(2)}, u32[]{:S(2)}) collective-permute-start(bf16[440,128]{1,0:T(8,128)(2,1)S(1)} %bitcast.15), channel_id=1, source_target_pairs={{0,16},{1,17},{2,18},{3,19},{4,20},{5,21},{6,22},{7,23},{8,24},{9,... | collective-permute-start | bytes 337928 | tf_op jit(solution)/shard_map/ppermute | solution.py:133
  8.7 1.6 %collective-permute-start.4 = (bf16[440,128]{1,0:T(8,128)(2,1)S(1)}, bf16[440,128]{1,0:T(8,128)(2,1)S(1)}, u32[]{:S(2)}, u32[]{:S(2)}) collective-permute-start(bf16[440,128]{1,0:T(8,128)(2,1)S(1)} %bitcast.16), channel_id=1, source_target_pairs={{0,8},{1,9},{2,10},{3,11},{4,12},{5,13},{6,14},{7,15},{8,0},{9,1},... | collective-permute-start | bytes 337928 | tf_op jit(solution)/shard_map/ppermute | solution.py:133
  10.2 2.4 %collective-permute-done.3.refs_4_ = bf16[440,128]{1,0:T(8,128)(2,1)S(1)} collective-permute-done((bf16[440,128]{1,0:T(8,128)(2,1)S(1)}, bf16[440,128]{1,0:T(8,128)(2,1)S(1)}, u32[]{:S(2)}, u32[]{:S(2)}) %collective-permute-start.3) | collective-permute-done | bytes 112672 | tf_op jit(solution)/shard_map/ppermute | solution.py:133
  12.6 0.0 collective-permute-start
  12.6 0.0 collective-permute-done.1.refs_2_.refs_11_
  12.6 0.5 %collective-permute-start.2 = (bf16[592,128]{1,0:T(8,128)(2,1)S(1)}, bf16[592,128]{1,0:T(8,128)(2,1)S(1)}, u32[]{:S(2)}, u32[]{:S(2)}) collective-permute-start(bf16[592,128]{1,0:T(8,128)(2,1)S(1)} %collective-permute-done.1.refs_2_.refs_11_), channel_id=1, source_target_pairs={{0,2},{1,3},{2,0},{3,1},{4,6},{5,7},{6,4},{7,5},{8,10},{9,11},{10,... | collective-permute-start | bytes 454664 | tf_op jit(solution)/shard_map/ppermute | solution.py:133
  13.2 0.0 collective-permute-done.5.refs_1_
  13.2 0.1 collective-permute-start.6
  13.2 0.0 collective-permute-done.7.refs_3_
  13.2 0.4 %collective-permute-start.8 = (bf16[592,128]{1,0:T(8,128)(2,1)S(1)}, bf16[592,128]{1,0:T(8,128)(2,1)S(1)}, u32[]{:S(2)}, u32[]{:S(2)}) collective-permute-start(bf16[592,128]{1,0:T(8,128)(2,1)S(1)} %collective-permute-done.7.refs_3_), channel_id=1, source_target_pairs={{0,2},{1,3},{2,0},{3,1},{4,6},{5,7},{6,4},{7,5},{8,10},{9,11},{10,... | collective-permute-start | bytes 454664 | tf_op jit(solution)/shard_map/ppermute | solution.py:133
  13.7 0.0 collective-permute-done.4.refs_5_
  13.7 1.5 %collective-permute-start.9 = (bf16[440,128]{1,0:T(8,128)(2,1)S(1)}, bf16[440,128]{1,0:T(8,128)(2,1)S(1)}, u32[]{:S(2)}, u32[]{:S(2)}) collective-permute-start(bf16[440,128]{1,0:T(8,128)(2,1)S(1)} %collective-permute-done.3.refs_4_), channel_id=1, source_target_pairs={{0,8},{1,9},{2,10},{3,11},{4,12},{5,13},{6,14},{7,15},{8,0},{9,1},... | collective-permute-start | bytes 337928 | tf_op jit(solution)/shard_map/ppermute | solution.py:133
  15.2 0.0 collective-permute-done.refs_1_.refs_10_
  15.2 0.0 collective-permute-done.2.refs_3_.refs_12_
  15.2 0.8 %products.3 = (f32[144,128]{1,0:T(8,128)S(1)}, f32[144,128]{1,0:T(8,128)S(1)}, f32[144,128]{1,0:T(8,128)S(1)}, bf16[128,448]{1,0:T(8,128)(2,1)S(1)}, bf16[128,44...) custom-call(bf16[592,128]{1,0:T(8,128)(2,1)S(1)} %stacked.1.refs_0_.refs_9_, ...), custom_call_target="tpu_custom_call" | custom-call | tf_op jit(solution)/shard_map/products/pallas_call | solution.py:117
  15.9 2.8 %collective-permute-done.9.refs_8_ = bf16[440,128]{1,0:T(8,128)(2,1)S(1)} collective-permute-done((bf16[440,128]{1,0:T(8,128)(2,1)S(1)}, bf16[440,128]{1,0:T(8,128)(2,1)S(1)}, u32[]{:S(2)}, u32[]{:S(2)}) %collective-permute-start.9) | collective-permute-done | bytes 112672 | tf_op jit(solution)/shard_map/ppermute | solution.py:133
  18.8 0.0 collective-permute-done.6.refs_2_
  18.8 0.0 collective-permute-done.8.refs_4_
  18.8 0.9 %products.5 = (bf16[144,128]{1,0:T(8,128)(2,1)S(1)}, bf16[144,128]{1,0:T(8,128)(2,1)S(1)}, bf16[144,128]{1,0:T(8,128)(2,1)S(1)}) custom-call(bf16[128,448]{1,0:T(8,128)(2,1)S(1)} %get-tuple-element.16.refs_0_, bf16[592,128]{1,0:T(8,128)(2,1)S(1)} %collective-permute-done.5.refs_1_, bf16[592,128]{1,0:T(8,128)(2,1)S(1)} %collective-permute-done.6.refs_2_, ...), custom_call_target="tpu_custom_call" | custom-call | tf_op jit(solution)/shard_map/products/pallas_call | solution.py:117
  19.7 4.3 %collective-permute-start.12 = (bf16[144,128]{1,0:T(8,128)(2,1)S(1)}, bf16[144,128]{1,0:T(8,128)(2,1)S(1)}, u32[]{:S(2)}, u32[]{:S(2)}) collective-permute-start(bf16[144,128]{1,0:T(8,128)(2,1)S(1)} %get-tuple-element.22), channel_id=1, source_target_pairs={{0,24},{1,25},{2,26},{3,27},{4,28},{5,29},{6,30},{7,31},{8,16},{9,... | collective-permute-start | bytes 110600 | tf_op jit(solution)/shard_map/ppermute | solution.py:133
  24.0 0.0 collective-permute-start.11
  24.0 0.6 %collective-permute-start.10 = (bf16[144,128]{1,0:T(8,128)(2,1)S(1)}, bf16[144,128]{1,0:T(8,128)(2,1)S(1)}, u32[]{:S(2)}, u32[]{:S(2)}) collective-permute-start(bf16[144,128]{1,0:T(8,128)(2,1)S(1)} %get-tuple-element.20), channel_id=1, source_target_pairs={{0,16},{1,17},{2,18},{3,19},{4,20},{5,21},{6,22},{7,23},{8,24},{9,... | collective-permute-start | bytes 110600 | tf_op jit(solution)/shard_map/ppermute | solution.py:133
  24.7 0.0 copy-start.1
  24.7 0.5 %products.4 = f32[144,128]{1,0:T(8,128)S(1)} custom-call(bf16[128,448]{1,0:T(8,128)(2,1)S(1)} %get-tuple-element.14.refs_0_, bf16[592,128]{1,0:T(8,128)(2,1)S(1)} %collective-permute-done.5.refs_1_, bf16[592,128]{1,0:T(8,128)(2,1)S(1)} %collective-permute-done.6.refs_2_, bf16[592,128]{1,0:T(8,128)(2,1)S(1)} %collective-permute-done.7.refs_3_, ...), custom_call_target="tpu_custom_call" | custom-call | tf_op jit(solution)/shard_map/products/pallas_call | solution.py:117
  25.2 0.9 %collective-permute-done.12 = bf16[144,128]{1,0:T(8,128)(2,1)S(1)} collective-permute-done((bf16[144,128]{1,0:T(8,128)(2,1)S(1)}, bf16[144,128]{1,0:T(8,128)(2,1)S(1)}, u32[]{:S(2)}, u32[]{:S(2)}) %collective-permute-start.12) | collective-permute-done | bytes 36896 | tf_op jit(solution)/shard_map/ppermute | solution.py:133
  26.1 1.9 %collective-permute-done.11 = bf16[144,128]{1,0:T(8,128)(2,1)S(1)} collective-permute-done((bf16[144,128]{1,0:T(8,128)(2,1)S(1)}, bf16[144,128]{1,0:T(8,128)(2,1)S(1)}, u32[]{:S(2)}, u32[]{:S(2)}) %collective-permute-start.11) | collective-permute-done | bytes 36896 | tf_op jit(solution)/shard_map/ppermute | solution.py:133
  28.0 0.9 %collective-permute-done.10 = bf16[144,128]{1,0:T(8,128)(2,1)S(1)} collective-permute-done((bf16[144,128]{1,0:T(8,128)(2,1)S(1)}, bf16[144,128]{1,0:T(8,128)(2,1)S(1)}, u32[]{:S(2)}, u32[]{:S(2)}) %collective-permute-start.10) | collective-permute-done | bytes 36896 | tf_op jit(solution)/shard_map/ppermute | solution.py:133
  28.9 0.0 copy-done.1
  28.9 0.7 %fusion.3 = f32[128,144]{0,1:T(8,128)} fusion(f32[144,128]{1,0:T(8,128)S(1)} %products.4, f32[128,144]{0,1:T(8,128)S(1)} %copy-done.1, bf16[144,128]{1,0:T(8,128)(2,1)S(1)} %collective-permute-done.12, bf16[144,128]{1,0:T(8,128)(2,1)S(1)} %collective-permute-done.11, bf16[144,128]{1,0:T(8,128)(2,1)S(1)} %collective-permute-done.10), kind=kLoop, calls=%fused_computation.4 | loop fusion | flops 129024 | bytes 331776 | tf_op jit(solution)/shard_map/transpose | solution.py:168
Async XLA Ops:
  0.0 5.7 %copy-start = (bf16[128,440]{0,1:T(8,128)(2,1)S(1)}, bf16[128,440]{0,1:T(8,128)(2,1)}, u32[]{:S(2)}) copy-start(bf16[128,440]{0,1:T(8,128)(2,1)} %param.3) | copy-start | bytes 337924
  1.1 11.6 %collective-permute-start.1 = (bf16[592,128]{1,0:T(8,128)(2,1)S(1)}, bf16[592,128]{1,0:T(8,128)(2,1)S(1)}, u32[]{:S(2)}, u32[]{:S(2)}) collective-permute-start(bf16[592,128]{1,0:T(8,128)(2,1)S(1)} %stacked.1.refs_0_.refs_9_), channel_id=1, source_target_pairs={{0,5},{1,4},{2,7},{3,6},{4,1},{5,0},{6,3},{7,2},{8,13},{9,12},{10,... | collective-permute-start | bytes 454664 | tf_op jit(solution)/shard_map/ppermute | solution.py:133
  5.0 8.1 %collective-permute-start.5 = (bf16[592,128]{1,0:T(8,128)(2,1)S(1)}, bf16[592,128]{1,0:T(8,128)(2,1)S(1)}, u32[]{:S(2)}, u32[]{:S(2)}) collective-permute-start(bf16[592,128]{1,0:T(8,128)(2,1)S(1)} %stacked.1.refs_0_.refs_9_), channel_id=1, source_target_pairs={{0,4},{1,5},{2,6},{3,7},{4,0},{5,1},{6,2},{7,3},{8,12},{9,13},{10,... | collective-permute-start | bytes 454664 | tf_op jit(solution)/shard_map/ppermute | solution.py:133
  5.6 7.7 %collective-permute-start.7 = (bf16[592,128]{1,0:T(8,128)(2,1)S(1)}, bf16[592,128]{1,0:T(8,128)(2,1)S(1)}, u32[]{:S(2)}, u32[]{:S(2)}) collective-permute-start(bf16[592,128]{1,0:T(8,128)(2,1)S(1)} %stacked.1.refs_0_.refs_9_), channel_id=1, source_target_pairs={{0,1},{1,0},{2,3},{3,2},{4,5},{5,4},{6,7},{7,6},{8,9},{9,8},{10,11... | collective-permute-start | bytes 454664 | tf_op jit(solution)/shard_map/ppermute | solution.py:133
  5.7 7.0 %collective-permute-start.3 = (bf16[440,128]{1,0:T(8,128)(2,1)S(1)}, bf16[440,128]{1,0:T(8,128)(2,1)S(1)}, u32[]{:S(2)}, u32[]{:S(2)}) collective-permute-start(bf16[440,128]{1,0:T(8,128)(2,1)S(1)} %bitcast.15), channel_id=1, source_target_pairs={{0,16},{1,17},{2,18},{3,19},{4,20},{5,21},{6,22},{7,23},{8,24},{9,... | collective-permute-start | bytes 337928 | tf_op jit(solution)/shard_map/ppermute | solution.py:133
  8.7 5.0 %collective-permute-start.4 = (bf16[440,128]{1,0:T(8,128)(2,1)S(1)}, bf16[440,128]{1,0:T(8,128)(2,1)S(1)}, u32[]{:S(2)}, u32[]{:S(2)}) collective-permute-start(bf16[440,128]{1,0:T(8,128)(2,1)S(1)} %bitcast.16), channel_id=1, source_target_pairs={{0,8},{1,9},{2,10},{3,11},{4,12},{5,13},{6,14},{7,15},{8,0},{9,1},... | collective-permute-start | bytes 337928 | tf_op jit(solution)/shard_map/ppermute | solution.py:133
  12.6 2.5 %collective-permute-start = (bf16[592,128]{1,0:T(8,128)(2,1)S(1)}, bf16[592,128]{1,0:T(8,128)(2,1)S(1)}, u32[]{:S(2)}, u32[]{:S(2)}) collective-permute-start(bf16[592,128]{1,0:T(8,128)(2,1)S(1)} %stacked.1.refs_0_.refs_9_), channel_id=1, source_target_pairs={{0,2},{1,3},{2,0},{3,1},{4,6},{5,7},{6,4},{7,5},{8,10},{9,11},{10,... | collective-permute-start | bytes 454664 | tf_op jit(solution)/shard_map/ppermute | solution.py:133
  12.6 2.5 %collective-permute-start.2 = (bf16[592,128]{1,0:T(8,128)(2,1)S(1)}, bf16[592,128]{1,0:T(8,128)(2,1)S(1)}, u32[]{:S(2)}, u32[]{:S(2)}) collective-permute-start(bf16[592,128]{1,0:T(8,128)(2,1)S(1)} %collective-permute-done.1.refs_2_.refs_11_), channel_id=1, source_target_pairs={{0,2},{1,3},{2,0},{3,1},{4,6},{5,7},{6,4},{7,5},{8,10},{9,11},{10,... | collective-permute-start | bytes 454664 | tf_op jit(solution)/shard_map/ppermute | solution.py:133
  13.2 5.6 %collective-permute-start.6 = (bf16[592,128]{1,0:T(8,128)(2,1)S(1)}, bf16[592,128]{1,0:T(8,128)(2,1)S(1)}, u32[]{:S(2)}, u32[]{:S(2)}) collective-permute-start(bf16[592,128]{1,0:T(8,128)(2,1)S(1)} %collective-permute-done.5.refs_1_), channel_id=1, source_target_pairs={{0,2},{1,3},{2,0},{3,1},{4,6},{5,7},{6,4},{7,5},{8,10},{9,11},{10,... | collective-permute-start | bytes 454664 | tf_op jit(solution)/shard_map/ppermute | solution.py:133
  13.2 5.5 %collective-permute-start.8 = (bf16[592,128]{1,0:T(8,128)(2,1)S(1)}, bf16[592,128]{1,0:T(8,128)(2,1)S(1)}, u32[]{:S(2)}, u32[]{:S(2)}) collective-permute-start(bf16[592,128]{1,0:T(8,128)(2,1)S(1)} %collective-permute-done.7.refs_3_), channel_id=1, source_target_pairs={{0,2},{1,3},{2,0},{3,1},{4,6},{5,7},{6,4},{7,5},{8,10},{9,11},{10,... | collective-permute-start | bytes 454664 | tf_op jit(solution)/shard_map/ppermute | solution.py:133
  13.7 5.1 %collective-permute-start.9 = (bf16[440,128]{1,0:T(8,128)(2,1)S(1)}, bf16[440,128]{1,0:T(8,128)(2,1)S(1)}, u32[]{:S(2)}, u32[]{:S(2)}) collective-permute-start(bf16[440,128]{1,0:T(8,128)(2,1)S(1)} %collective-permute-done.3.refs_4_), channel_id=1, source_target_pairs={{0,8},{1,9},{2,10},{3,11},{4,12},{5,13},{6,14},{7,15},{8,0},{9,1},... | collective-permute-start | bytes 337928 | tf_op jit(solution)/shard_map/ppermute | solution.py:133
  19.7 6.4 %collective-permute-start.12 = (bf16[144,128]{1,0:T(8,128)(2,1)S(1)}, bf16[144,128]{1,0:T(8,128)(2,1)S(1)}, u32[]{:S(2)}, u32[]{:S(2)}) collective-permute-start(bf16[144,128]{1,0:T(8,128)(2,1)S(1)} %get-tuple-element.22), channel_id=1, source_target_pairs={{0,24},{1,25},{2,26},{3,27},{4,28},{5,29},{6,30},{7,31},{8,16},{9,... | collective-permute-start | bytes 110600 | tf_op jit(solution)/shard_map/ppermute | solution.py:133
  24.0 4.0 %collective-permute-start.11 = (bf16[144,128]{1,0:T(8,128)(2,1)S(1)}, bf16[144,128]{1,0:T(8,128)(2,1)S(1)}, u32[]{:S(2)}, u32[]{:S(2)}) collective-permute-start(bf16[144,128]{1,0:T(8,128)(2,1)S(1)} %get-tuple-element.21), channel_id=1, source_target_pairs={{0,8},{1,9},{2,10},{3,11},{4,12},{5,13},{6,14},{7,15},{8,0},{9,1},... | collective-permute-start | bytes 110600 | tf_op jit(solution)/shard_map/ppermute | solution.py:133
  24.0 4.9 %collective-permute-start.10 = (bf16[144,128]{1,0:T(8,128)(2,1)S(1)}, bf16[144,128]{1,0:T(8,128)(2,1)S(1)}, u32[]{:S(2)}, u32[]{:S(2)}) collective-permute-start(bf16[144,128]{1,0:T(8,128)(2,1)S(1)} %get-tuple-element.20), channel_id=1, source_target_pairs={{0,16},{1,17},{2,18},{3,19},{4,20},{5,21},{6,22},{7,23},{8,24},{9,... | collective-permute-start | bytes 110600 | tf_op jit(solution)/shard_map/ppermute | solution.py:133
  24.7 4.2 %copy-start.1 = (f32[128,144]{0,1:T(8,128)S(1)}, f32[128,144]{0,1:T(8,128)}, u32[]{:S(2)}) copy-start(f32[128,144]{0,1:T(8,128)} %param.5) | copy-start | bytes 221188

commit v3 on v2

--- a/solution.py
+++ b/solution.py
@@ -45,7 +45,7 @@
     )(weights, values)
 
 
-def products(work, outs, feats, kinds, near, prepared=0):
+def products(work, outs, feats, kinds, near, prepared=0, minus=None):
     arrays, slots = [], {}
 
     def slot(a):
@@ -63,6 +63,7 @@
         )
         for q, keys, old in work
     ]
+    taken = None if minus is None else slot(minus)
     count, entries = len(arrays), len(work)
     width = work[0][1][0].shape[1]
 
@@ -104,6 +105,7 @@
             total = acc[i].T
             old = plan[i][3]
             total = total if old is None else total + ins[old][...]
+            total = total if taken is None else total - ins[taken][...]
             out_refs[i][...] = total.astype(out_refs[i].dtype)
 
     shapes = [((outs, width), kind) for kind in kinds]
@@ -161,8 +163,7 @@
     sent = [(q, keys[half:], e) for q, e in zip(ready, early)][1:]
     sent = sent + [(q, keys, None) for q in queries[len(lead):]]
     parts = run(sent, kinds=[b16] * len(sent)) if sent else []
-    own = run([(ready[0], keys[half:], early[0])], kinds=[f32])[0]
-    result = own - targets.T
+    result = run([(ready[0], keys[half:], early[0])], kinds=[f32], minus=targets.T)[0]
     for n, part in enumerate(parts):
         result = result + swap(part, order[n + 1]).astype(f32)
     return result.T

time: 29.7 us -> 31.1 us (1.047)
  waiting for transfers between devices: 8.93 us -> 10.5 us
    ppermute x13, waiting for transfers between devices: 8.93 us -> 10.5 us  [swap(): return lax.ppermute(value, AXES, [(i, i ^ bits) for i in range(total)])]
  transfers between devices with their start and end apart: 13 -> 13, of which waited for: 5 -> 4; matrix products, arithmetic and copies ran while one was open for 0% -> 0% of each run, Pallas kernels for 4% -> 4%
where the time goes in v3:
time: 31.1 us; the launch traced here: 31 us
  starting transfers between devices  16.6 us (53%)
  waiting for transfers between devices  10.5 us (34%)
  Pallas kernels  3.26 us (10%)
  other arithmetic  0.65 us (2%)
    ppermute x13, starting transfers between devices, swap(): return lax.ppermute(value, AXES, [(i, i ^ bits) for i in range(total)])  16.6 us
    ppermute x13, waiting for transfers between devices, swap(): return lax.ppermute(value, AXES, [(i, i ^ bits) for i in range(total)])  10.5 us
    pallas_call x3, Pallas kernels, products(): pl.pallas_call(body, out_shape=shapes, in_specs=[vmem] * count, out_specs...  2.21 us
    pallas_call x1, Pallas kernels, stacked(): pl.pallas_call(body, out_shape=pltpu.VMEM(shape, values.dtype) if near el...  1.05 us
    transpose x1, other arithmetic, per_device(): return result.T  0.65 us
  transfers between devices with their start and end apart: 13, of which 4 were waited for; matrix products, arithmetic and copies ran while one was open for 0% of the time, Pallas kernels for 4%

profile of v3, /device:TPU:0, one launch (start us, length us, event | category | flops | bytes accessed | tf_op | source)
XLA Modules:
  0.0 31.0 jit_solution(2716308303235955845)
XLA Ops:
  0.0 0.0 copy-start.1
  0.0 1.1 %stacked.1.refs_0_.refs_9_ = bf16[592,128]{1,0:T(8,128)(2,1)S(1)} custom-call(bf16[144,128]{1,0:T(8,128)(2,1)} %bitcast.9, bf16[440,128]{1,0:T(8,128)(2,1)} %bitcast.6), custom_call_target="tpu_custom_call" | custom-call | tf_op jit(solution)/shard_map/stacked/pallas_call | solution.py:39
  1.1 4.0 %collective-permute-start.1 = (bf16[592,128]{1,0:T(8,128)(2,1)S(1)}, bf16[592,128]{1,0:T(8,128)(2,1)S(1)}, u32[]{:S(2)}, u32[]{:S(2)}) collective-permute-start(bf16[592,128]{1,0:T(8,128)(2,1)S(1)} %stacked.1.refs_0_.refs_9_), channel_id=1, source_target_pairs={{0,5},{1,4},{2,7},{3,6},{4,1},{5,0},{6,3},{7,2},{8,13},{9,12},{10,... | collective-permute-start | bytes 454664 | tf_op jit(solution)/shard_map/ppermute | solution.py:135
  5.0 0.5 %collective-permute-start.5 = (bf16[592,128]{1,0:T(8,128)(2,1)S(1)}, bf16[592,128]{1,0:T(8,128)(2,1)S(1)}, u32[]{:S(2)}, u32[]{:S(2)}) collective-permute-start(bf16[592,128]{1,0:T(8,128)(2,1)S(1)} %stacked.1.refs_0_.refs_9_), channel_id=1, source_target_pairs={{0,4},{1,5},{2,6},{3,7},{4,0},{5,1},{6,2},{7,3},{8,12},{9,13},{10,... | collective-permute-start | bytes 454664 | tf_op jit(solution)/shard_map/ppermute | solution.py:135
  5.6 0.1 collective-permute-start.7
  5.7 0.0 copy-done.1
  5.7 3.0 %collective-permute-start.3 = (bf16[440,128]{1,0:T(8,128)(2,1)S(1)}, bf16[440,128]{1,0:T(8,128)(2,1)S(1)}, u32[]{:S(2)}, u32[]{:S(2)}) collective-permute-start(bf16[440,128]{1,0:T(8,128)(2,1)S(1)} %bitcast.7), channel_id=1, source_target_pairs={{0,16},{1,17},{2,18},{3,19},{4,20},{5,21},{6,22},{7,23},{8,24},{9,... | collective-permute-start | bytes 337928 | tf_op jit(solution)/shard_map/ppermute | solution.py:135
  8.7 1.6 %collective-permute-start.4 = (bf16[440,128]{1,0:T(8,128)(2,1)S(1)}, bf16[440,128]{1,0:T(8,128)(2,1)S(1)}, u32[]{:S(2)}, u32[]{:S(2)}) collective-permute-start(bf16[440,128]{1,0:T(8,128)(2,1)S(1)} %bitcast.8), channel_id=1, source_target_pairs={{0,8},{1,9},{2,10},{3,11},{4,12},{5,13},{6,14},{7,15},{8,0},{9,1},... | collective-permute-start | bytes 337928 | tf_op jit(solution)/shard_map/ppermute | solution.py:135
  10.2 2.4 %collective-permute-done.3.refs_4_ = bf16[440,128]{1,0:T(8,128)(2,1)S(1)} collective-permute-done((bf16[440,128]{1,0:T(8,128)(2,1)S(1)}, bf16[440,128]{1,0:T(8,128)(2,1)S(1)}, u32[]{:S(2)}, u32[]{:S(2)}) %collective-permute-start.3) | collective-permute-done | bytes 112672 | tf_op jit(solution)/shard_map/ppermute | solution.py:135
  12.6 0.0 collective-permute-start
  12.6 0.0 collective-permute-done.1.refs_2_.refs_11_
  12.6 0.5 %collective-permute-start.2 = (bf16[592,128]{1,0:T(8,128)(2,1)S(1)}, bf16[592,128]{1,0:T(8,128)(2,1)S(1)}, u32[]{:S(2)}, u32[]{:S(2)}) collective-permute-start(bf16[592,128]{1,0:T(8,128)(2,1)S(1)} %collective-permute-done.1.refs_2_.refs_11_), channel_id=1, source_target_pairs={{0,2},{1,3},{2,0},{3,1},{4,6},{5,7},{6,4},{7,5},{8,10},{9,11},{10,... | collective-permute-start | bytes 454664 | tf_op jit(solution)/shard_map/ppermute | solution.py:135
  13.2 0.0 collective-permute-done.5.refs_1_
  13.2 0.1 collective-permute-start.6
  13.2 0.0 collective-permute-done.7.refs_3_
  13.2 0.4 %collective-permute-start.8 = (bf16[592,128]{1,0:T(8,128)(2,1)S(1)}, bf16[592,128]{1,0:T(8,128)(2,1)S(1)}, u32[]{:S(2)}, u32[]{:S(2)}) collective-permute-start(bf16[592,128]{1,0:T(8,128)(2,1)S(1)} %collective-permute-done.7.refs_3_), channel_id=1, source_target_pairs={{0,2},{1,3},{2,0},{3,1},{4,6},{5,7},{6,4},{7,5},{8,10},{9,11},{10,... | collective-permute-start | bytes 454664 | tf_op jit(solution)/shard_map/ppermute | solution.py:135
  13.7 0.0 collective-permute-done.4.refs_5_
  13.7 1.5 %collective-permute-start.9 = (bf16[440,128]{1,0:T(8,128)(2,1)S(1)}, bf16[440,128]{1,0:T(8,128)(2,1)S(1)}, u32[]{:S(2)}, u32[]{:S(2)}) collective-permute-start(bf16[440,128]{1,0:T(8,128)(2,1)S(1)} %collective-permute-done.3.refs_4_), channel_id=1, source_target_pairs={{0,8},{1,9},{2,10},{3,11},{4,12},{5,13},{6,14},{7,15},{8,0},{9,1},... | collective-permute-start | bytes 337928 | tf_op jit(solution)/shard_map/ppermute | solution.py:135
  15.2 0.0 collective-permute-done.refs_1_.refs_10_
  15.2 0.0 collective-permute-done.2.refs_3_.refs_12_
  15.2 0.8 %products.3 = (f32[144,128]{1,0:T(8,128)S(1)}, f32[144,128]{1,0:T(8,128)S(1)}, f32[144,128]{1,0:T(8,128)S(1)}, bf16[128,448]{1,0:T(8,128)(2,1)S(1)}, bf16[128,44...) custom-call(bf16[592,128]{1,0:T(8,128)(2,1)S(1)} %stacked.1.refs_0_.refs_9_, ...), custom_call_target="tpu_custom_call" | custom-call | tf_op jit(solution)/shard_map/products/pallas_call | solution.py:119
  15.9 2.8 %collective-permute-done.9.refs_8_ = bf16[440,128]{1,0:T(8,128)(2,1)S(1)} collective-permute-done((bf16[440,128]{1,0:T(8,128)(2,1)S(1)}, bf16[440,128]{1,0:T(8,128)(2,1)S(1)}, u32[]{:S(2)}, u32[]{:S(2)}) %collective-permute-start.9) | collective-permute-done | bytes 112672 | tf_op jit(solution)/shard_map/ppermute | solution.py:135
  18.8 0.0 collective-permute-done.6.refs_2_
  18.8 0.0 collective-permute-done.8.refs_4_
  18.8 0.0 copy-start
  18.8 1.0 %products.5 = (bf16[144,128]{1,0:T(8,128)(2,1)S(1)}, bf16[144,128]{1,0:T(8,128)(2,1)S(1)}, bf16[144,128]{1,0:T(8,128)(2,1)S(1)}) custom-call(bf16[128,448]{1,0:T(8,128)(2,1)S(1)} %get-tuple-element.16.refs_0_, bf16[592,128]{1,0:T(8,128)(2,1)S(1)} %collective-permute-done.5.refs_1_, bf16[592,128]{1,0:T(8,128)(2,1)S(1)} %collective-permute-done.6.refs_2_, ...), custom_call_target="tpu_custom_call" | custom-call | tf_op jit(solution)/shard_map/products/pallas_call | solution.py:119
  19.7 3.1 %collective-permute-start.10 = (bf16[144,128]{1,0:T(8,128)(2,1)S(1)}, bf16[144,128]{1,0:T(8,128)(2,1)S(1)}, u32[]{:S(2)}, u32[]{:S(2)}) collective-permute-start(bf16[144,128]{1,0:T(8,128)(2,1)S(1)} %get-tuple-element.20), channel_id=1, source_target_pairs={{0,16},{1,17},{2,18},{3,19},{4,20},{5,21},{6,22},{7,23},{8,24},{9,... | collective-permute-start | bytes 110600 | tf_op jit(solution)/shard_map/ppermute | solution.py:135
  22.9 1.7 %collective-permute-start.11 = (bf16[144,128]{1,0:T(8,128)(2,1)S(1)}, bf16[144,128]{1,0:T(8,128)(2,1)S(1)}, u32[]{:S(2)}, u32[]{:S(2)}) collective-permute-start(bf16[144,128]{1,0:T(8,128)(2,1)S(1)} %get-tuple-element.21), channel_id=1, source_target_pairs={{0,8},{1,9},{2,10},{3,11},{4,12},{5,13},{6,14},{7,15},{8,0},{9,1},... | collective-permute-start | bytes 110600 | tf_op jit(solution)/shard_map/ppermute | solution.py:135
  24.6 0.0 collective-permute-start.12
  24.6 0.0 copy-done
  24.6 0.5 %products.4 = f32[144,128]{1,0:T(8,128)S(1)} custom-call(bf16[128,448]{1,0:T(8,128)(2,1)S(1)} %get-tuple-element.14.refs_0_, bf16[592,128]{1,0:T(8,128)(2,1)S(1)} %collective-permute-done.5.refs_1_, bf16[592,128]{1,0:T(8,128)(2,1)S(1)} %collective-permute-done.6.refs_2_, bf16[592,128]{1,0:T(8,128)(2,1)S(1)} %collective-permute-done.7.refs_3_, ...), custom_call_target="tpu_custom_call" | custom-call | tf_op jit(solution)/shard_map/products/pallas_call | solution.py:119
  25.1 0.0 collective-permute-done.10
  25.1 1.7 %collective-permute-done.11 = bf16[144,128]{1,0:T(8,128)(2,1)S(1)} collective-permute-done((bf16[144,128]{1,0:T(8,128)(2,1)S(1)}, bf16[144,128]{1,0:T(8,128)(2,1)S(1)}, u32[]{:S(2)}, u32[]{:S(2)}) %collective-permute-start.11) | collective-permute-done | bytes 36896 | tf_op jit(solution)/shard_map/ppermute | solution.py:135
  26.8 3.5 %collective-permute-done.12 = bf16[144,128]{1,0:T(8,128)(2,1)S(1)} collective-permute-done((bf16[144,128]{1,0:T(8,128)(2,1)S(1)}, bf16[144,128]{1,0:T(8,128)(2,1)S(1)}, u32[]{:S(2)}, u32[]{:S(2)}) %collective-permute-start.12) | collective-permute-done | bytes 36896 | tf_op jit(solution)/shard_map/ppermute | solution.py:135
  30.4 0.7 %add_bitcast_fusion = f32[128,144]{0,1:T(8,128)} fusion(bf16[144,128]{1,0:T(8,128)(2,1)S(1)} %collective-permute-done.12, bf16[144,128]{1,0:T(8,128)(2,1)S(1)} %collective-permute-done.11, f32[144,128]{1,0:T(8,128)S(1)} %products.4, bf16[144,128]{1,0:T(8,128)(2,1)S(1)} %collective-permute-done.10), kind=kLoop, calls=%fused_computation | loop fusion | flops 110592 | bytes 258048 | tf_op jit(solution)/shard_map/transpose | solution.py:169
Async XLA Ops:
  0.0 5.7 %copy-start.1 = (bf16[128,440]{0,1:T(8,128)(2,1)S(1)}, bf16[128,440]{0,1:T(8,128)(2,1)}, u32[]{:S(2)}) copy-start(bf16[128,440]{0,1:T(8,128)(2,1)} %param.3) | copy-start | bytes 337924
  1.1 11.6 %collective-permute-start.1 = (bf16[592,128]{1,0:T(8,128)(2,1)S(1)}, bf16[592,128]{1,0:T(8,128)(2,1)S(1)}, u32[]{:S(2)}, u32[]{:S(2)}) collective-permute-start(bf16[592,128]{1,0:T(8,128)(2,1)S(1)} %stacked.1.refs_0_.refs_9_), channel_id=1, source_target_pairs={{0,5},{1,4},{2,7},{3,6},{4,1},{5,0},{6,3},{7,2},{8,13},{9,12},{10,... | collective-permute-start | bytes 454664 | tf_op jit(solution)/shard_map/ppermute | solution.py:135
  5.0 8.1 %collective-permute-start.5 = (bf16[592,128]{1,0:T(8,128)(2,1)S(1)}, bf16[592,128]{1,0:T(8,128)(2,1)S(1)}, u32[]{:S(2)}, u32[]{:S(2)}) collective-permute-start(bf16[592,128]{1,0:T(8,128)(2,1)S(1)} %stacked.1.refs_0_.refs_9_), channel_id=1, source_target_pairs={{0,4},{1,5},{2,6},{3,7},{4,0},{5,1},{6,2},{7,3},{8,12},{9,13},{10,... | collective-permute-start | bytes 454664 | tf_op jit(solution)/shard_map/ppermute | solution.py:135
  5.6 7.7 %collective-permute-start.7 = (bf16[592,128]{1,0:T(8,128)(2,1)S(1)}, bf16[592,128]{1,0:T(8,128)(2,1)S(1)}, u32[]{:S(2)}, u32[]{:S(2)}) collective-permute-start(bf16[592,128]{1,0:T(8,128)(2,1)S(1)} %stacked.1.refs_0_.refs_9_), channel_id=1, source_target_pairs={{0,1},{1,0},{2,3},{3,2},{4,5},{5,4},{6,7},{7,6},{8,9},{9,8},{10,11... | collective-permute-start | bytes 454664 | tf_op jit(solution)/shard_map/ppermute | solution.py:135
  5.7 7.0 %collective-permute-start.3 = (bf16[440,128]{1,0:T(8,128)(2,1)S(1)}, bf16[440,128]{1,0:T(8,128)(2,1)S(1)}, u32[]{:S(2)}, u32[]{:S(2)}) collective-permute-start(bf16[440,128]{1,0:T(8,128)(2,1)S(1)} %bitcast.7), channel_id=1, source_target_pairs={{0,16},{1,17},{2,18},{3,19},{4,20},{5,21},{6,22},{7,23},{8,24},{9,... | collective-permute-start | bytes 337928 | tf_op jit(solution)/shard_map/ppermute | solution.py:135
  8.7 5.0 %collective-permute-start.4 = (bf16[440,128]{1,0:T(8,128)(2,1)S(1)}, bf16[440,128]{1,0:T(8,128)(2,1)S(1)}, u32[]{:S(2)}, u32[]{:S(2)}) collective-permute-start(bf16[440,128]{1,0:T(8,128)(2,1)S(1)} %bitcast.8), channel_id=1, source_target_pairs={{0,8},{1,9},{2,10},{3,11},{4,12},{5,13},{6,14},{7,15},{8,0},{9,1},... | collective-permute-start | bytes 337928 | tf_op jit(solution)/shard_map/ppermute | solution.py:135
  12.6 2.5 %collective-permute-start = (bf16[592,128]{1,0:T(8,128)(2,1)S(1)}, bf16[592,128]{1,0:T(8,128)(2,1)S(1)}, u32[]{:S(2)}, u32[]{:S(2)}) collective-permute-start(bf16[592,128]{1,0:T(8,128)(2,1)S(1)} %stacked.1.refs_0_.refs_9_), channel_id=1, source_target_pairs={{0,2},{1,3},{2,0},{3,1},{4,6},{5,7},{6,4},{7,5},{8,10},{9,11},{10,... | collective-permute-start | bytes 454664 | tf_op jit(solution)/shard_map/ppermute | solution.py:135
  12.6 2.5 %collective-permute-start.2 = (bf16[592,128]{1,0:T(8,128)(2,1)S(1)}, bf16[592,128]{1,0:T(8,128)(2,1)S(1)}, u32[]{:S(2)}, u32[]{:S(2)}) collective-permute-start(bf16[592,128]{1,0:T(8,128)(2,1)S(1)} %collective-permute-done.1.refs_2_.refs_11_), channel_id=1, source_target_pairs={{0,2},{1,3},{2,0},{3,1},{4,6},{5,7},{6,4},{7,5},{8,10},{9,11},{10,... | collective-permute-start | bytes 454664 | tf_op jit(solution)/shard_map/ppermute | solution.py:135
  13.2 5.6 %collective-permute-start.6 = (bf16[592,128]{1,0:T(8,128)(2,1)S(1)}, bf16[592,128]{1,0:T(8,128)(2,1)S(1)}, u32[]{:S(2)}, u32[]{:S(2)}) collective-permute-start(bf16[592,128]{1,0:T(8,128)(2,1)S(1)} %collective-permute-done.5.refs_1_), channel_id=1, source_target_pairs={{0,2},{1,3},{2,0},{3,1},{4,6},{5,7},{6,4},{7,5},{8,10},{9,11},{10,... | collective-permute-start | bytes 454664 | tf_op jit(solution)/shard_map/ppermute | solution.py:135
  13.2 5.5 %collective-permute-start.8 = (bf16[592,128]{1,0:T(8,128)(2,1)S(1)}, bf16[592,128]{1,0:T(8,128)(2,1)S(1)}, u32[]{:S(2)}, u32[]{:S(2)}) collective-permute-start(bf16[592,128]{1,0:T(8,128)(2,1)S(1)} %collective-permute-done.7.refs_3_), channel_id=1, source_target_pairs={{0,2},{1,3},{2,0},{3,1},{4,6},{5,7},{6,4},{7,5},{8,10},{9,11},{10,... | collective-permute-start | bytes 454664 | tf_op jit(solution)/shard_map/ppermute | solution.py:135
  13.7 5.1 %collective-permute-start.9 = (bf16[440,128]{1,0:T(8,128)(2,1)S(1)}, bf16[440,128]{1,0:T(8,128)(2,1)S(1)}, u32[]{:S(2)}, u32[]{:S(2)}) collective-permute-start(bf16[440,128]{1,0:T(8,128)(2,1)S(1)} %collective-permute-done.3.refs_4_), channel_id=1, source_target_pairs={{0,8},{1,9},{2,10},{3,11},{4,12},{5,13},{6,14},{7,15},{8,0},{9,1},... | collective-permute-start | bytes 337928 | tf_op jit(solution)/shard_map/ppermute | solution.py:135
  18.8 5.8 %copy-start = (f32[128,144]{0,1:T(8,128)S(1)}, f32[128,144]{0,1:T(8,128)}, u32[]{:S(2)}) copy-start(f32[128,144]{0,1:T(8,128)} %param.5) | copy-start | bytes 221188
  19.7 5.4 %collective-permute-start.10 = (bf16[144,128]{1,0:T(8,128)(2,1)S(1)}, bf16[144,128]{1,0:T(8,128)(2,1)S(1)}, u32[]{:S(2)}, u32[]{:S(2)}) collective-permute-start(bf16[144,128]{1,0:T(8,128)(2,1)S(1)} %get-tuple-element.20), channel_id=1, source_target_pairs={{0,16},{1,17},{2,18},{3,19},{4,20},{5,21},{6,22},{7,23},{8,24},{9,... | collective-permute-start | bytes 110600 | tf_op jit(solution)/shard_map/ppermute | solution.py:135
  22.9 4.0 %collective-permute-start.11 = (bf16[144,128]{1,0:T(8,128)(2,1)S(1)}, bf16[144,128]{1,0:T(8,128)(2,1)S(1)}, u32[]{:S(2)}, u32[]{:S(2)}) collective-permute-start(bf16[144,128]{1,0:T(8,128)(2,1)S(1)} %get-tuple-element.21), channel_id=1, source_target_pairs={{0,8},{1,9},{2,10},{3,11},{4,12},{5,13},{6,14},{7,15},{8,0},{9,1},... | collective-permute-start | bytes 110600 | tf_op jit(solution)/shard_map/ppermute | solution.py:135
  24.6 5.8 %collective-permute-start.12 = (bf16[144,128]{1,0:T(8,128)(2,1)S(1)}, bf16[144,128]{1,0:T(8,128)(2,1)S(1)}, u32[]{:S(2)}, u32[]{:S(2)}) collective-permute-start(bf16[144,128]{1,0:T(8,128)(2,1)S(1)} %get-tuple-element.22), channel_id=1, source_target_pairs={{0,24},{1,25},{2,26},{3,27},{4,28},{5,29},{6,30},{7,31},{8,16},{9,... | collective-permute-start | bytes 110600 | tf_op jit(solution)/shard_map/ppermute | solution.py:135

commit v4 on v3

--- a/solution.py
+++ b/solution.py
@@ -148,8 +148,10 @@
     queries[0] = both
     blocks = [both]
     for plane in reversed(range(1, 2 * cols)):
-        bits = (plane // cols) * xbit + plane % cols
-        blocks.append(swap(both, bits))
+        other = plane if plane == 2 * cols - 1 else 2 * cols - 1 - plane
+        bits = [(p // cols) * xbit + p % cols for p in (plane, other)]
+        pairs = [(i, i ^ bits[i // core % 2]) for i in range(total)]
+        blocks.append(lax.ppermute(both, AXES, pairs))
     keys = []
     for b in blocks:
         keys = keys + [b, swap(b, core)]

time: 31.1 us -> 31.1 us (level)
    ppermute x0 -> x3, starting transfers between devices: none -> 4.62 us  [per_device(): blocks.append(lax.ppermute(both, AXES, pairs))]
    ppermute x13 -> x10, starting transfers between devices: 16.6 us -> 12 us  [swap(): return lax.ppermute(value, AXES, [(i, i ^ bits) for i in range(total)])]
    ppermute x13 -> x10, waiting for transfers between devices: 10.5 us -> 10.4 us  [swap(): return lax.ppermute(value, AXES, [(i, i ^ bits) for i in range(total)])]
where the time goes in v4:
time: 31.1 us; the launch traced here: 31 us
  starting transfers between devices  16.6 us (53%)
  waiting for transfers between devices  10.5 us (34%)
  Pallas kernels  3.26 us (10%)
  other arithmetic  0.65 us (2%)
    ppermute x10, starting transfers between devices, swap(): return lax.ppermute(value, AXES, [(i, i ^ bits) for i in range(total)])  12 us
    ppermute x10, waiting for transfers between devices, swap(): return lax.ppermute(value, AXES, [(i, i ^ bits) for i in range(total)])  10.4 us
    ppermute x3, starting transfers between devices, per_device(): blocks.append(lax.ppermute(both, AXES, pairs))  4.62 us
    pallas_call x3, Pallas kernels, products(): pl.pallas_call(body, out_shape=shapes, in_specs=[vmem] * count, out_specs...  2.21 us
    pallas_call x1, Pallas kernels, stacked(): pl.pallas_call(body, out_shape=pltpu.VMEM(shape, values.dtype) if near el...  1.05 us
    transpose x1, other arithmetic, per_device(): return result.T  0.65 us
  transfers between devices with their start and end apart: 13, of which 4 were waited for; matrix products, arithmetic and copies ran while one was open for 0% of the time, Pallas kernels for 4%

profile of v4, /device:TPU:0, one launch (start us, length us, event | category | flops | bytes accessed | tf_op | source)
XLA Modules:
  0.0 31.0 jit_solution(2829712120902762625)
XLA Ops:
  0.0 0.0 copy-start.1
  0.0 1.1 %stacked.1.refs_0_.refs_9_ = bf16[592,128]{1,0:T(8,128)(2,1)S(1)} custom-call(bf16[144,128]{1,0:T(8,128)(2,1)} %bitcast.9, bf16[440,128]{1,0:T(8,128)(2,1)} %bitcast.6), custom_call_target="tpu_custom_call" | custom-call | tf_op jit(solution)/shard_map/stacked/pallas_call | solution.py:39
  1.1 4.0 %collective-permute-start.1 = (bf16[592,128]{1,0:T(8,128)(2,1)S(1)}, bf16[592,128]{1,0:T(8,128)(2,1)S(1)}, u32[]{:S(2)}, u32[]{:S(2)}) collective-permute-start(bf16[592,128]{1,0:T(8,128)(2,1)S(1)} %stacked.1.refs_0_.refs_9_), channel_id=1, source_target_pairs={{0,5},{1,4},{2,7},{3,6},{4,1},{5,0},{6,3},{7,2},{8,13},{9,12},{10,... | collective-permute-start | bytes 454664 | tf_op jit(solution)/shard_map/ppermute | solution.py:154
  5.0 0.5 %collective-permute-start.5 = (bf16[592,128]{1,0:T(8,128)(2,1)S(1)}, bf16[592,128]{1,0:T(8,128)(2,1)S(1)}, u32[]{:S(2)}, u32[]{:S(2)}) collective-permute-start(bf16[592,128]{1,0:T(8,128)(2,1)S(1)} %stacked.1.refs_0_.refs_9_), channel_id=1, source_target_pairs={{0,4},{1,5},{2,3},{3,2},{4,0},{5,1},{6,7},{7,6},{8,12},{9,13},{10,... | collective-permute-start | bytes 454664 | tf_op jit(solution)/shard_map/ppermute | solution.py:154
  5.6 0.1 collective-permute-start.7
  5.7 0.0 copy-done.1
  5.7 3.0 %collective-permute-start.3 = (bf16[440,128]{1,0:T(8,128)(2,1)S(1)}, bf16[440,128]{1,0:T(8,128)(2,1)S(1)}, u32[]{:S(2)}, u32[]{:S(2)}) collective-permute-start(bf16[440,128]{1,0:T(8,128)(2,1)S(1)} %bitcast.7), channel_id=1, source_target_pairs={{0,16},{1,17},{2,18},{3,19},{4,20},{5,21},{6,22},{7,23},{8,24},{9,... | collective-permute-start | bytes 337928 | tf_op jit(solution)/shard_map/ppermute | solution.py:135
  8.7 1.6 %collective-permute-start.4 = (bf16[440,128]{1,0:T(8,128)(2,1)S(1)}, bf16[440,128]{1,0:T(8,128)(2,1)S(1)}, u32[]{:S(2)}, u32[]{:S(2)}) collective-permute-start(bf16[440,128]{1,0:T(8,128)(2,1)S(1)} %bitcast.8), channel_id=1, source_target_pairs={{0,8},{1,9},{2,10},{3,11},{4,12},{5,13},{6,14},{7,15},{8,0},{9,1},... | collective-permute-start | bytes 337928 | tf_op jit(solution)/shard_map/ppermute | solution.py:135
  10.2 2.4 %collective-permute-done.3.refs_4_ = bf16[440,128]{1,0:T(8,128)(2,1)S(1)} collective-permute-done((bf16[440,128]{1,0:T(8,128)(2,1)S(1)}, bf16[440,128]{1,0:T(8,128)(2,1)S(1)}, u32[]{:S(2)}, u32[]{:S(2)}) %collective-permute-start.3) | collective-permute-done | bytes 112672 | tf_op jit(solution)/shard_map/ppermute | solution.py:135
  12.6 0.0 collective-permute-start
  12.6 0.0 collective-permute-done.1.refs_2_.refs_11_
  12.6 0.5 %collective-permute-start.2 = (bf16[592,128]{1,0:T(8,128)(2,1)S(1)}, bf16[592,128]{1,0:T(8,128)(2,1)S(1)}, u32[]{:S(2)}, u32[]{:S(2)}) collective-permute-start(bf16[592,128]{1,0:T(8,128)(2,1)S(1)} %collective-permute-done.1.refs_2_.refs_11_), channel_id=1, source_target_pairs={{0,2},{1,3},{2,0},{3,1},{4,6},{5,7},{6,4},{7,5},{8,10},{9,11},{10,... | collective-permute-start | bytes 454664 | tf_op jit(solution)/shard_map/ppermute | solution.py:135
  13.2 0.0 collective-permute-done.5.refs_1_
  13.2 0.1 collective-permute-start.6
  13.2 0.0 collective-permute-done.7.refs_3_
  13.2 0.4 %collective-permute-start.8 = (bf16[592,128]{1,0:T(8,128)(2,1)S(1)}, bf16[592,128]{1,0:T(8,128)(2,1)S(1)}, u32[]{:S(2)}, u32[]{:S(2)}) collective-permute-start(bf16[592,128]{1,0:T(8,128)(2,1)S(1)} %collective-permute-done.7.refs_3_), channel_id=1, source_target_pairs={{0,2},{1,3},{2,0},{3,1},{4,6},{5,7},{6,4},{7,5},{8,10},{9,11},{10,... | collective-permute-start | bytes 454664 | tf_op jit(solution)/shard_map/ppermute | solution.py:135
  13.7 0.0 collective-permute-done.4.refs_5_
  13.7 1.5 %collective-permute-start.9 = (bf16[440,128]{1,0:T(8,128)(2,1)S(1)}, bf16[440,128]{1,0:T(8,128)(2,1)S(1)}, u32[]{:S(2)}, u32[]{:S(2)}) collective-permute-start(bf16[440,128]{1,0:T(8,128)(2,1)S(1)} %collective-permute-done.3.refs_4_), channel_id=1, source_target_pairs={{0,8},{1,9},{2,10},{3,11},{4,12},{5,13},{6,14},{7,15},{8,0},{9,1},... | collective-permute-start | bytes 337928 | tf_op jit(solution)/shard_map/ppermute | solution.py:135
  15.2 0.0 collective-permute-done.refs_1_.refs_10_
  15.2 0.0 collective-permute-done.2.refs_3_.refs_12_
  15.2 0.8 %products.3 = (f32[144,128]{1,0:T(8,128)S(1)}, f32[144,128]{1,0:T(8,128)S(1)}, f32[144,128]{1,0:T(8,128)S(1)}, bf16[128,448]{1,0:T(8,128)(2,1)S(1)}, bf16[128,44...) custom-call(bf16[592,128]{1,0:T(8,128)(2,1)S(1)} %stacked.1.refs_0_.refs_9_, ...), custom_call_target="tpu_custom_call" | custom-call | tf_op jit(solution)/shard_map/products/pallas_call | solution.py:119
  15.9 2.8 %collective-permute-done.9.refs_8_ = bf16[440,128]{1,0:T(8,128)(2,1)S(1)} collective-permute-done((bf16[440,128]{1,0:T(8,128)(2,1)S(1)}, bf16[440,128]{1,0:T(8,128)(2,1)S(1)}, u32[]{:S(2)}, u32[]{:S(2)}) %collective-permute-start.9) | collective-permute-done | bytes 112672 | tf_op jit(solution)/shard_map/ppermute | solution.py:135
  18.8 0.0 collective-permute-done.6.refs_2_
  18.8 0.0 collective-permute-done.8.refs_4_
  18.8 0.0 copy-start
  18.8 1.0 %products.5 = (bf16[144,128]{1,0:T(8,128)(2,1)S(1)}, bf16[144,128]{1,0:T(8,128)(2,1)S(1)}, bf16[144,128]{1,0:T(8,128)(2,1)S(1)}) custom-call(bf16[128,448]{1,0:T(8,128)(2,1)S(1)} %get-tuple-element.16.refs_0_, bf16[592,128]{1,0:T(8,128)(2,1)S(1)} %collective-permute-done.5.refs_1_, bf16[592,128]{1,0:T(8,128)(2,1)S(1)} %collective-permute-done.6.refs_2_, ...), custom_call_target="tpu_custom_call" | custom-call | tf_op jit(solution)/shard_map/products/pallas_call | solution.py:119
  19.7 3.1 %collective-permute-start.10 = (bf16[144,128]{1,0:T(8,128)(2,1)S(1)}, bf16[144,128]{1,0:T(8,128)(2,1)S(1)}, u32[]{:S(2)}, u32[]{:S(2)}) collective-permute-start(bf16[144,128]{1,0:T(8,128)(2,1)S(1)} %get-tuple-element.20), channel_id=1, source_target_pairs={{0,16},{1,17},{2,18},{3,19},{4,20},{5,21},{6,22},{7,23},{8,24},{9,... | collective-permute-start | bytes 110600 | tf_op jit(solution)/shard_map/ppermute | solution.py:135
  22.9 1.7 %collective-permute-start.11 = (bf16[144,128]{1,0:T(8,128)(2,1)S(1)}, bf16[144,128]{1,0:T(8,128)(2,1)S(1)}, u32[]{:S(2)}, u32[]{:S(2)}) collective-permute-start(bf16[144,128]{1,0:T(8,128)(2,1)S(1)} %get-tuple-element.21), channel_id=1, source_target_pairs={{0,8},{1,9},{2,10},{3,11},{4,12},{5,13},{6,14},{7,15},{8,0},{9,1},... | collective-permute-start | bytes 110600 | tf_op jit(solution)/shard_map/ppermute | solution.py:135
  24.6 0.0 collective-permute-start.12
  24.6 0.0 copy-done
  24.6 0.5 %products.4 = f32[144,128]{1,0:T(8,128)S(1)} custom-call(bf16[128,448]{1,0:T(8,128)(2,1)S(1)} %get-tuple-element.14.refs_0_, bf16[592,128]{1,0:T(8,128)(2,1)S(1)} %collective-permute-done.5.refs_1_, bf16[592,128]{1,0:T(8,128)(2,1)S(1)} %collective-permute-done.6.refs_2_, bf16[592,128]{1,0:T(8,128)(2,1)S(1)} %collective-permute-done.7.refs_3_, ...), custom_call_target="tpu_custom_call" | custom-call | tf_op jit(solution)/shard_map/products/pallas_call | solution.py:119
  25.1 0.0 collective-permute-done.10
  25.1 1.7 %collective-permute-done.11 = bf16[144,128]{1,0:T(8,128)(2,1)S(1)} collective-permute-done((bf16[144,128]{1,0:T(8,128)(2,1)S(1)}, bf16[144,128]{1,0:T(8,128)(2,1)S(1)}, u32[]{:S(2)}, u32[]{:S(2)}) %collective-permute-start.11) | collective-permute-done | bytes 36896 | tf_op jit(solution)/shard_map/ppermute | solution.py:135
  26.8 3.5 %collective-permute-done.12 = bf16[144,128]{1,0:T(8,128)(2,1)S(1)} collective-permute-done((bf16[144,128]{1,0:T(8,128)(2,1)S(1)}, bf16[144,128]{1,0:T(8,128)(2,1)S(1)}, u32[]{:S(2)}, u32[]{:S(2)}) %collective-permute-start.12) | collective-permute-done | bytes 36896 | tf_op jit(solution)/shard_map/ppermute | solution.py:135
  30.4 0.7 %add_bitcast_fusion = f32[128,144]{0,1:T(8,128)} fusion(bf16[144,128]{1,0:T(8,128)(2,1)S(1)} %collective-permute-done.12, bf16[144,128]{1,0:T(8,128)(2,1)S(1)} %collective-permute-done.11, f32[144,128]{1,0:T(8,128)S(1)} %products.4, bf16[144,128]{1,0:T(8,128)(2,1)S(1)} %collective-permute-done.10), kind=kLoop, calls=%fused_computation | loop fusion | flops 110592 | bytes 258048 | tf_op jit(solution)/shard_map/transpose | solution.py:171
Async XLA Ops:
  0.0 5.7 %copy-start.1 = (bf16[128,440]{0,1:T(8,128)(2,1)S(1)}, bf16[128,440]{0,1:T(8,128)(2,1)}, u32[]{:S(2)}) copy-start(bf16[128,440]{0,1:T(8,128)(2,1)} %param.3) | copy-start | bytes 337924
  1.1 11.6 %collective-permute-start.1 = (bf16[592,128]{1,0:T(8,128)(2,1)S(1)}, bf16[592,128]{1,0:T(8,128)(2,1)S(1)}, u32[]{:S(2)}, u32[]{:S(2)}) collective-permute-start(bf16[592,128]{1,0:T(8,128)(2,1)S(1)} %stacked.1.refs_0_.refs_9_), channel_id=1, source_target_pairs={{0,5},{1,4},{2,7},{3,6},{4,1},{5,0},{6,3},{7,2},{8,13},{9,12},{10,... | collective-permute-start | bytes 454664 | tf_op jit(solution)/shard_map/ppermute | solution.py:154
  5.0 8.1 %collective-permute-start.5 = (bf16[592,128]{1,0:T(8,128)(2,1)S(1)}, bf16[592,128]{1,0:T(8,128)(2,1)S(1)}, u32[]{:S(2)}, u32[]{:S(2)}) collective-permute-start(bf16[592,128]{1,0:T(8,128)(2,1)S(1)} %stacked.1.refs_0_.refs_9_), channel_id=1, source_target_pairs={{0,4},{1,5},{2,3},{3,2},{4,0},{5,1},{6,7},{7,6},{8,12},{9,13},{10,... | collective-permute-start | bytes 454664 | tf_op jit(solution)/shard_map/ppermute | solution.py:154
  5.6 7.7 %collective-permute-start.7 = (bf16[592,128]{1,0:T(8,128)(2,1)S(1)}, bf16[592,128]{1,0:T(8,128)(2,1)S(1)}, u32[]{:S(2)}, u32[]{:S(2)}) collective-permute-start(bf16[592,128]{1,0:T(8,128)(2,1)S(1)} %stacked.1.refs_0_.refs_9_), channel_id=1, source_target_pairs={{0,1},{1,0},{2,6},{3,7},{4,5},{5,4},{6,2},{7,3},{8,9},{9,8},{10,14... | collective-permute-start | bytes 454664 | tf_op jit(solution)/shard_map/ppermute | solution.py:154
  5.7 7.0 %collective-permute-start.3 = (bf16[440,128]{1,0:T(8,128)(2,1)S(1)}, bf16[440,128]{1,0:T(8,128)(2,1)S(1)}, u32[]{:S(2)}, u32[]{:S(2)}) collective-permute-start(bf16[440,128]{1,0:T(8,128)(2,1)S(1)} %bitcast.7), channel_id=1, source_target_pairs={{0,16},{1,17},{2,18},{3,19},{4,20},{5,21},{6,22},{7,23},{8,24},{9,... | collective-permute-start | bytes 337928 | tf_op jit(solution)/shard_map/ppermute | solution.py:135
  8.7 5.0 %collective-permute-start.4 = (bf16[440,128]{1,0:T(8,128)(2,1)S(1)}, bf16[440,128]{1,0:T(8,128)(2,1)S(1)}, u32[]{:S(2)}, u32[]{:S(2)}) collective-permute-start(bf16[440,128]{1,0:T(8,128)(2,1)S(1)} %bitcast.8), channel_id=1, source_target_pairs={{0,8},{1,9},{2,10},{3,11},{4,12},{5,13},{6,14},{7,15},{8,0},{9,1},... | collective-permute-start | bytes 337928 | tf_op jit(solution)/shard_map/ppermute | solution.py:135
  12.6 2.5 %collective-permute-start = (bf16[592,128]{1,0:T(8,128)(2,1)S(1)}, bf16[592,128]{1,0:T(8,128)(2,1)S(1)}, u32[]{:S(2)}, u32[]{:S(2)}) collective-permute-start(bf16[592,128]{1,0:T(8,128)(2,1)S(1)} %stacked.1.refs_0_.refs_9_), channel_id=1, source_target_pairs={{0,2},{1,3},{2,0},{3,1},{4,6},{5,7},{6,4},{7,5},{8,10},{9,11},{10,... | collective-permute-start | bytes 454664 | tf_op jit(solution)/shard_map/ppermute | solution.py:135
  12.6 2.5 %collective-permute-start.2 = (bf16[592,128]{1,0:T(8,128)(2,1)S(1)}, bf16[592,128]{1,0:T(8,128)(2,1)S(1)}, u32[]{:S(2)}, u32[]{:S(2)}) collective-permute-start(bf16[592,128]{1,0:T(8,128)(2,1)S(1)} %collective-permute-done.1.refs_2_.refs_11_), channel_id=1, source_target_pairs={{0,2},{1,3},{2,0},{3,1},{4,6},{5,7},{6,4},{7,5},{8,10},{9,11},{10,... | collective-permute-start | bytes 454664 | tf_op jit(solution)/shard_map/ppermute | solution.py:135
  13.2 5.6 %collective-permute-start.6 = (bf16[592,128]{1,0:T(8,128)(2,1)S(1)}, bf16[592,128]{1,0:T(8,128)(2,1)S(1)}, u32[]{:S(2)}, u32[]{:S(2)}) collective-permute-start(bf16[592,128]{1,0:T(8,128)(2,1)S(1)} %collective-permute-done.5.refs_1_), channel_id=1, source_target_pairs={{0,2},{1,3},{2,0},{3,1},{4,6},{5,7},{6,4},{7,5},{8,10},{9,11},{10,... | collective-permute-start | bytes 454664 | tf_op jit(solution)/shard_map/ppermute | solution.py:135
  13.2 5.5 %collective-permute-start.8 = (bf16[592,128]{1,0:T(8,128)(2,1)S(1)}, bf16[592,128]{1,0:T(8,128)(2,1)S(1)}, u32[]{:S(2)}, u32[]{:S(2)}) collective-permute-start(bf16[592,128]{1,0:T(8,128)(2,1)S(1)} %collective-permute-done.7.refs_3_), channel_id=1, source_target_pairs={{0,2},{1,3},{2,0},{3,1},{4,6},{5,7},{6,4},{7,5},{8,10},{9,11},{10,... | collective-permute-start | bytes 454664 | tf_op jit(solution)/shard_map/ppermute | solution.py:135
  13.7 5.1 %collective-permute-start.9 = (bf16[440,128]{1,0:T(8,128)(2,1)S(1)}, bf16[440,128]{1,0:T(8,128)(2,1)S(1)}, u32[]{:S(2)}, u32[]{:S(2)}) collective-permute-start(bf16[440,128]{1,0:T(8,128)(2,1)S(1)} %collective-permute-done.3.refs_4_), channel_id=1, source_target_pairs={{0,8},{1,9},{2,10},{3,11},{4,12},{5,13},{6,14},{7,15},{8,0},{9,1},... | collective-permute-start | bytes 337928 | tf_op jit(solution)/shard_map/ppermute | solution.py:135
  18.8 5.8 %copy-start = (f32[128,144]{0,1:T(8,128)S(1)}, f32[128,144]{0,1:T(8,128)}, u32[]{:S(2)}) copy-start(f32[128,144]{0,1:T(8,128)} %param.5) | copy-start | bytes 221188
  19.7 5.4 %collective-permute-start.10 = (bf16[144,128]{1,0:T(8,128)(2,1)S(1)}, bf16[144,128]{1,0:T(8,128)(2,1)S(1)}, u32[]{:S(2)}, u32[]{:S(2)}) collective-permute-start(bf16[144,128]{1,0:T(8,128)(2,1)S(1)} %get-tuple-element.20), channel_id=1, source_target_pairs={{0,16},{1,17},{2,18},{3,19},{4,20},{5,21},{6,22},{7,23},{8,24},{9,... | collective-permute-start | bytes 110600 | tf_op jit(solution)/shard_map/ppermute | solution.py:135
  22.9 4.0 %collective-permute-start.11 = (bf16[144,128]{1,0:T(8,128)(2,1)S(1)}, bf16[144,128]{1,0:T(8,128)(2,1)S(1)}, u32[]{:S(2)}, u32[]{:S(2)}) collective-permute-start(bf16[144,128]{1,0:T(8,128)(2,1)S(1)} %get-tuple-element.21), channel_id=1, source_target_pairs={{0,8},{1,9},{2,10},{3,11},{4,12},{5,13},{6,14},{7,15},{8,0},{9,1},... | collective-permute-start | bytes 110600 | tf_op jit(solution)/shard_map/ppermute | solution.py:135
  24.6 5.8 %collective-permute-start.12 = (bf16[144,128]{1,0:T(8,128)(2,1)S(1)}, bf16[144,128]{1,0:T(8,128)(2,1)S(1)}, u32[]{:S(2)}, u32[]{:S(2)}) collective-permute-start(bf16[144,128]{1,0:T(8,128)(2,1)S(1)} %get-tuple-element.22), channel_id=1, source_target_pairs={{0,24},{1,25},{2,26},{3,27},{4,28},{5,29},{6,30},{7,31},{8,16},{9,... | collective-permute-start | bytes 110600 | tf_op jit(solution)/shard_map/ppermute | solution.py:135
